TPU v7x, 256 devices: a 4x2x16 block of a 4x16x16 slice. The times are simulated.
256 devices in a mesh: kgrp: 2 (over y), band: 16 (over z), fft: 8 (over x, core).
Axes of the slice: x: 4, y: 2, z: 16, core: 2. Of those that a mesh axis runs over, the one named last changes fastest.
The devices are a block of a 4x16x16 slice.
Arguments:
- orbitals: float32 [32, 64, 64, 128], P(('kgrp', 'band'), 'fft'), parts along dimension 0, may hold values from -6 to 6
- partners: float32 [32, 64, 64, 128], P(('kgrp', 'band'), 'fft'), parts along dimension 0, may hold values from -6 to 6
- shift_table: float32 [8, 3], replicated, may hold values from -0.5 to 0.5
- shift_index: int32 [32], P('kgrp'), parts along dimension 0, may hold values from 0 to 7
Outputs:
- potential: float32 [32, 64, 64, 128], P(('kgrp', 'band'), 'fft'), parts along dimension 0
- projector: float32 [32, 64, 64, 128], P(('kgrp', 'band'), 'fft'), parts along dimension 0
There are 2 independent parts, one for each index of `kgrp`. A program takes and returns all parts, laid end to end along the dimension named above; an argument that names none is the same for every part. Nothing has to cross between parts.
All inputs are finite; a program needn't handle non-finite values.
Results may differ from a plain program's by a relative error of at most 0.0001.
Values sent between devices are 32-bit elements; how exact they have to be, the bound alone decides.
A program may use at most 64 MiB of HBM per device.

v0:
```python
import math

import jax
import jax.numpy as jnp
from jax import lax
from jax.sharding import PartitionSpec as P

HIGHEST = lax.Precision.HIGHEST
SCREEN_SQUARE = 0.25
FOUR_PI = 4.0 * math.pi


def copy_for_each(x, axis):
    peers = lax.axis_size(axis)
    return lax.all_to_all(jnp.broadcast_to(x[None], (peers, *x.shape)), axis, 0, 0, tiled=True)


def joined_along(pieces, dim):
    dims = list(pieces.shape[1:])
    dims[dim] *= pieces.shape[0]
    return jnp.moveaxis(pieces, 0, dim).reshape(dims)


def collect(x, axis, dim):
    pieces = copy_for_each(x, axis)
    return joined_along(pieces, dim)


def cut_along(x, dim, peers):
    before, after = (x.shape[:dim], x.shape[dim + 1 :])
    return jnp.moveaxis(x.reshape(*before, peers, -1, *after), dim, 0)


def summed_on_arrival(x, axis, dim):
    pieces = cut_along(x, dim, lax.axis_size(axis))
    arrived = lax.all_to_all(pieces, axis, split_axis=0, concat_axis=0, tiled=True)
    return arrived.sum(axis=0)


def of_everyone(x, axis):
    return copy_for_each(x, axis).sum(axis=0)


def together(arrays, axis):
    vector, at, done = (jnp.concatenate([a.reshape(-1) for a in arrays]), 0, [])
    so_far = of_everyone(vector, axis)
    for a in arrays:
        done.append(so_far[at : at + a.size].reshape(a.shape))
        at += a.size
    return tuple(done)


def in_one_piece(arrays, axis, dim, along):
    widths = [a.shape[along] for a in arrays]
    both = jnp.concatenate(arrays, axis=along)
    out = lax.all_gather(both, axis, axis=dim, tiled=True)
    return tuple(jnp.split(out, [sum(widths[:k]) for k in range(1, len(widths))], axis=along))


def angle_pair(extent, sign):
    positions = jnp.arange(extent, dtype=jnp.int32)
    product = positions[:, None] * positions[None, :] % extent
    angle = 2.0 * math.pi / extent * product.astype(jnp.float32)
    return (jnp.cos(angle), sign * jnp.sin(angle))


def last_table(extent, sign):
    cosine, sine = angle_pair(extent, sign)
    upper = jnp.concatenate([cosine, sine], axis=1)
    lower = jnp.concatenate([-sine, cosine], axis=1)
    return jnp.concatenate([upper, lower], axis=0)


def middle_table(extent, sign):
    cosine, sine = angle_pair(extent, sign)
    return jnp.stack([jnp.stack([cosine, -sine], -1), jnp.stack([sine, cosine], -1)], 1)


def along_last(field, table):
    shape = field.shape
    flat = field.reshape(-1, shape[-1])
    return jnp.dot(flat, table, precision=HIGHEST).reshape(shape)


def along_axis(field, table, axis_number):
    shape = field.shape
    extent = shape[-1] // 2
    split = field.reshape(shape[0], shape[1], shape[2], 2, extent)
    if axis_number == 1:
        result = jnp.einsum("kcnd,pnbdz->pkbcz", table, split, precision=HIGHEST)
    else:
        result = jnp.einsum("kcnd,pandz->pakcz", table, split, precision=HIGHEST)
    return result.reshape(shape)


def times_conj(left, right):
    extent = left.shape[-1] // 2
    left_real, left_imag = (left[..., :extent], left[..., extent:])
    right_real, right_imag = (right[..., :extent], right[..., extent:])
    return jnp.concatenate(
        [
            left_real * right_real + left_imag * right_imag,
            left_real * right_imag - left_imag * right_real,
        ],
        axis=-1,
    )


def times(left, right):
    extent = left.shape[-1] // 2
    left_real, left_imag = (left[..., :extent], left[..., extent:])
    right_real, right_imag = (right[..., :extent], right[..., extent:])
    return jnp.concatenate(
        [
            left_real * right_real - left_imag * right_imag,
            left_real * right_imag + left_imag * right_real,
        ],
        axis=-1,
    )


def rotate(field):
    extent = field.shape[-1] // 2
    return jnp.concatenate([field[..., extent:], -field[..., :extent]], axis=-1)


def frequency(positions, extent):
    return jnp.where(positions < extent // 2, positions, positions - extent).astype(jnp.float32)


def kernel_block(qvectors, y_count, extent):
    first_freq = frequency(jnp.arange(extent, dtype=jnp.int32), extent)
    second_freq = frequency(jnp.arange(y_count, dtype=jnp.int32), extent)
    third_freq = frequency(jnp.arange(2 * extent, dtype=jnp.int32) % extent, extent)
    first_part = (first_freq[None, :] + qvectors[:, 0:1]) ** 2
    second_part = (second_freq[None, :] + qvectors[:, 1:2]) ** 2
    third_part = (third_freq[None, :] + qvectors[:, 2:3]) ** 2
    denominator = (
        first_part[:, :, None, None]
        + second_part[:, None, :, None]
        + third_part[:, None, None, :]
        + SCREEN_SQUARE
    )
    return FOUR_PI / extent**3 / denominator


def shifts_for(shift_table, shift_index, start_at, length):
    picked = lax.dynamic_slice_in_dim(shift_index, start_at, length)
    onehot = (picked[:, None] == jnp.arange(shift_table.shape[0], dtype=jnp.int32)[None, :]).astype(
        jnp.float32
    )
    return jnp.dot(onehot, shift_table, precision=HIGHEST)


def factor_inverse(over_real, over_imag):
    matrix_order = over_real.shape[0]
    positions = jnp.arange(matrix_order, dtype=jnp.int32)
    zero_start = jnp.zeros_like(over_real)

    def chol_step(column, lowers):
        lower_real, lower_imag = lowers
        row_real = lower_real[column]
        row_imag = lower_imag[column]
        resid_real = over_real[:, column] - (
            jnp.dot(lower_real, row_real, precision=HIGHEST)
            + jnp.dot(lower_imag, row_imag, precision=HIGHEST)
        )
        resid_imag = over_imag[:, column] - (
            jnp.dot(lower_imag, row_real, precision=HIGHEST)
            - jnp.dot(lower_real, row_imag, precision=HIGHEST)
        )
        pivot_value = jnp.sqrt(resid_real[column])
        below_diag = positions > column
        at_diag = positions == column
        new_real = jnp.where(
            below_diag, resid_real / pivot_value, jnp.where(at_diag, pivot_value, 0.0)
        )
        new_imag = jnp.where(below_diag, resid_imag / pivot_value, 0.0)
        chosen = positions[None, :] == column
        return (
            jnp.where(chosen, new_real[:, None], lower_real),
            jnp.where(chosen, new_imag[:, None], lower_imag),
        )

    lower_real, lower_imag = lax.fori_loop(0, matrix_order, chol_step, (zero_start, zero_start))

    def solve_step(row_index, inverses):
        inv_real, inv_imag = inverses
        row_real = lower_real[row_index]
        row_imag = lower_imag[row_index]
        sum_real = jnp.dot(row_real, inv_real, precision=HIGHEST) - jnp.dot(
            row_imag, inv_imag, precision=HIGHEST
        )
        sum_imag = jnp.dot(row_real, inv_imag, precision=HIGHEST) + jnp.dot(
            row_imag, inv_real, precision=HIGHEST
        )
        unit_row = (positions == row_index).astype(over_real.dtype)
        pivot_value = lower_real[row_index, row_index]
        new_real = (unit_row - sum_real) / pivot_value
        new_imag = -sum_imag / pivot_value
        chosen = positions[:, None] == row_index
        return (
            jnp.where(chosen, new_real[None, :], inv_real),
            jnp.where(chosen, new_imag[None, :], inv_imag),
        )

    return lax.fori_loop(0, matrix_order, solve_step, (zero_start, zero_start))


def body(orbitals, partners, shift_table, shift_index):
    extent = orbitals.shape[2]
    band_count = orbitals.shape[0]
    tables = (
        last_table(extent, -1.0),
        middle_table(extent, -1.0),
        last_table(extent, 1.0),
        middle_table(extent, 1.0),
    )
    my_band = lax.axis_index("band")
    forward_last, forward_mid, inverse_last, inverse_mid = tables
    full_orbitals = collect(orbitals, "fft", 1)
    every_slab = lax.all_gather(partners, "band", axis=0, tiled=True)
    own_grids = lax.all_to_all(every_slab, "fft", split_axis=0, concat_axis=1, tiled=True)
    own_count = own_grids.shape[0]
    qvectors = shifts_for(shift_table, shift_index, lax.axis_index("fft") * own_count, own_count)

    def one_partner(member, running):
        single = lax.dynamic_slice_in_dim(own_grids, member, 1, 0)
        kernel = kernel_block(lax.dynamic_slice_in_dim(qvectors, member, 1, 0), extent, extent)
        density = times_conj(single, full_orbitals)
        spectrum = (
            along_axis(
                along_axis(along_last(density, forward_last), forward_mid, 2), forward_mid, 1
            )
            * kernel
        )
        field = along_last(
            along_axis(along_axis(spectrum, inverse_mid, 1), inverse_mid, 2), inverse_last
        )
        return running + times(single, field)

    partial_value = lax.fori_loop(
        0, own_count, one_partner, jnp.zeros(full_orbitals.shape, jnp.float32)
    )
    potential = summed_on_arrival(partial_value, "fft", 1)
    every_pot = lax.all_gather(potential, "band", axis=0, tiled=True)
    turned = rotate(every_pot)
    total_bands = every_pot.shape[0]
    flat_orbitals = orbitals.reshape(band_count, -1)
    flat_pot = every_pot.reshape(total_bands, -1)
    flat_turned = turned.reshape(total_bands, -1)
    volume = float(extent**3)
    rows_real = jnp.einsum("ik,jk->ij", flat_orbitals, flat_pot, precision=HIGHEST) / volume
    rows_imag = jnp.einsum("ik,jk->ij", flat_orbitals, flat_turned, precision=HIGHEST) / volume
    start_row = my_band * band_count
    summed_real, summed_imag = together((rows_real, rows_imag), "fft")
    over_real, over_imag = in_one_piece((summed_real, summed_imag), "band", 0, 1)
    inv_real, inv_imag = factor_inverse(over_real, over_imag)
    coef_real = lax.dynamic_slice_in_dim(inv_real, start_row, band_count, 0)
    coef_imag = lax.dynamic_slice_in_dim(inv_imag, start_row, band_count, 0)
    projector = jnp.dot(coef_real, flat_pot, precision=HIGHEST) + jnp.dot(
        coef_imag, flat_turned, precision=HIGHEST
    )
    return (potential, projector.reshape(orbitals.shape))


def solution(mesh):
    in_specs = (
        P(("kgrp", "band"), "fft", None, None),
        P(("kgrp", "band"), "fft", None, None),
        P(),
        P("kgrp"),
    )
    out_specs = (P(("kgrp", "band"), "fft", None, None), P(("kgrp", "band"), "fft", None, None))
    return jax.shard_map(body, mesh=mesh, in_specs=in_specs, out_specs=out_specs, check_vma=False)
```

profile of v0, /device:TPU:33, one launch (start us, length us, event | category | flops | bytes accessed | tf_op | source)
XLA Modules:
  0.0 575.5 jit_solution(6875662935293470920)
XLA Ops:
  8.0 83.7 %all-gather.5.cloned.1.call-done = f32[16,8,64,128]{3,2,1,0:T(8,128)} async-done(((f32[1,8,64,128]{3,2,1,0:T(8,128)}), f32[16,8,64,128]{3,2,1,0:T(8,128)}) %all-gather.5.cloned.1.call-update) | async-done | bytes 4194320 | tf_op jit(solution)/shard_map/all_gather | solution.py:222
  91.7 62.9 %all_to_all.34 = f32[16,8,64,128]{3,2,1,0:T(8,128)} all-to-all(f32[16,8,64,128]{3,2,1,0:T(8,128)} %all-gather.5.cloned.1.call-done), channel_id=1, replica_groups=mesh['kgrp'=2,'band'=16,'fft'=8] {'fft'}, dimensions={0} | all-to-all | bytes 8388608 | tf_op jit(solution)/shard_map/all_to_all | solution.py:223
  167.3 19.8 %all-to-all-done.1 = f32[8,1,8,64,128]{4,3,2,1,0:T(8,128)S(1)} async-done(((f32[8,1,8,64,128]{4,3,2,1,0:T(8,128)}), f32[8,1,8,64,128]{4,3,2,1,0:T(8,128)S(1)}, u32[]{:S(2)}, u32[]{:S(2)}) %all-to-all-start.1) | async-done | bytes 2097184 | tf_op jit(solution)/shard_map/all_to_all | solution.py:15
  187.1 139.2 %while.50 = (s32[]{:T(128)}, f32[1,64,64,128]{3,2,1,0:T(8,128)}, f32[2,64,64,128]{3,2,1,0:T(8,128)}, f32[1,64,64,128]{3,2,1,0:T(8,128)S(1)}, f32[128,128]{0,1:T(...) while((s32[]{:T(128)}, f32[1,64,64,128]{3,2,1,0:T(8,128)}, ...), condition=%wide.region_1.2_spmd.clone, body=%wide.region_0.1_spmd.clone.sunk | while | flops 4839185408 | bytes 69634296 | solution.py:242
  208.5 6.6 %fusion.194 = f32[64,64,2,64]{1,3,2,0:T(8,128)S(1)} fusion(f32[2,64,128,1]{2,1,0,3:T(8,128)S(1)} %bitcast.328, f32[1,64,64,64]{3,2,1,0:T(8,128)S(1)} %get-tuple-element.820, f32[1,64,64,64]{3,2,1,0:T(8,128)S(1)} %get-tuple-element.821), kind=kOutput, calls=%fused_computation.13.clone.1 | convolution fusion | flops 805830656 | bytes 4259840 | tf_op jit(solution)/shard_map/while/body/eval_jaxpr/dot_general | solution.py:82
  220.2 6.1 %copy.74 = f32[64,64,2,64,1]{0,3,2,4,1:T(8,128)} copy(f32[64,64,2,64,1]{1,3,2,0,4:T(8,128)} %fusion.195) | data formatting | bytes 4194304 | tf_op jit(solution)/shard_map/reshape.358
  226.3 5.8 %fusion.196 = f32[64,64,64,2,1]{2,1,4,3,0:T(8,128)S(1)} fusion(f32[64,64,2,64,1]{0,3,2,4,1:T(8,128)} %copy.74, f32[64,2,64,2]{2,0,3,1:T(8,128)S(1)} %get-tuple-element.874), kind=kOutput, calls=%fused_computation.29.clone.1 | convolution fusion | flops 805306368 | bytes 4259840 | tf_op jit(solution)/shard_map/while/body/eval_jaxpr/kcnd,pnbdz->pkbcz/dot_general | solution.py:90
  238.4 6.1 %copy.75 = f32[64,64,2,64,1]{1,3,2,4,0:T(8,128)} copy(f32[64,64,2,64,1]{0,3,2,1,4:T(8,128)} %fusion.199) | data formatting | bytes 4194304 | tf_op jit(solution)/shard_map/reshape.365
  244.5 5.8 %fusion.200 = f32[64,64,64,2,1]{2,1,4,3,0:T(8,128)S(1)} fusion(f32[64,64,2,64,1]{1,3,2,4,0:T(8,128)} %copy.75, f32[64,2,64,2]{2,0,3,1:T(8,128)S(1)} %get-tuple-element.876), kind=kOutput, calls=%fused_computation.26.clone.1 | convolution fusion | flops 805306368 | bytes 4259840 | tf_op jit(solution)/shard_map/while/body/eval_jaxpr/kcnd,pandz->pakcz/dot_general | solution.py:92
  250.3 6.7 %convolution_bitcast_fusion.15 = f32[1,64,64,128]{3,2,1,0:T(8,128)S(1)} fusion(f32[64,64,128]{1,2,0:T(8,128)S(1)} %bitcast.321, f32[128,128]{1,0:T(8,128)S(1)} %get-tuple-element.877), kind=kOutput, calls=%fused_computation.25.clone.1 | convolution fusion | flops 805306368 | bytes 4259840 | tf_op jit(solution)/shard_map/while/body/eval_jaxpr/dot_general | solution.py:82
  269.8 6.5 %fusion.194 = f32[64,64,2,64]{1,3,2,0:T(8,128)S(1)} fusion(f32[2,64,128,1]{2,1,0,3:T(8,128)S(1)} %bitcast.328, f32[1,64,64,64]{3,2,1,0:T(8,128)S(1)} %get-tuple-element.820, f32[1,64,64,64]{3,2,1,0:T(8,128)S(1)} %get-tuple-element.821), kind=kOutput, calls=%fused_computation.13.clone.1 | convolution fusion | flops 805830656 | bytes 4259840 | tf_op jit(solution)/shard_map/while/body/eval_jaxpr/dot_general | solution.py:82
  281.5 6.1 %copy.74 = f32[64,64,2,64,1]{0,3,2,4,1:T(8,128)} copy(f32[64,64,2,64,1]{1,3,2,0,4:T(8,128)} %fusion.195) | data formatting | bytes 4194304 | tf_op jit(solution)/shard_map/reshape.358
  287.5 5.8 %fusion.196 = f32[64,64,64,2,1]{2,1,4,3,0:T(8,128)S(1)} fusion(f32[64,64,2,64,1]{0,3,2,4,1:T(8,128)} %copy.74, f32[64,2,64,2]{2,0,3,1:T(8,128)S(1)} %get-tuple-element.874), kind=kOutput, calls=%fused_computation.29.clone.1 | convolution fusion | flops 805306368 | bytes 4259840 | tf_op jit(solution)/shard_map/while/body/eval_jaxpr/kcnd,pnbdz->pkbcz/dot_general | solution.py:90
  299.6 6.1 %copy.75 = f32[64,64,2,64,1]{1,3,2,4,0:T(8,128)} copy(f32[64,64,2,64,1]{0,3,2,1,4:T(8,128)} %fusion.199) | data formatting | bytes 4194304 | tf_op jit(solution)/shard_map/reshape.365
  311.5 6.7 %convolution_bitcast_fusion.15 = f32[1,64,64,128]{3,2,1,0:T(8,128)S(1)} fusion(f32[64,64,128]{1,2,0:T(8,128)S(1)} %bitcast.321, f32[128,128]{1,0:T(8,128)S(1)} %get-tuple-element.877), kind=kOutput, calls=%fused_computation.25.clone.1 | convolution fusion | flops 805306368 | bytes 4259840 | tf_op jit(solution)/shard_map/while/body/eval_jaxpr/dot_general | solution.py:82
  326.3 30.6 %all_to_all.35 = f32[8,1,8,64,128]{4,3,2,1,0:T(8,128)S(1)} all-to-all(f32[8,1,8,64,128]{4,3,2,1,0:T(8,128)} %bitcast.323), channel_id=1, replica_groups=mesh['kgrp'=2,'band'=16,'fft'=8] {'fft'}, dimensions={0} | all-to-all | bytes 4194304 | tf_op jit(solution)/shard_map/all_to_all | solution.py:36
  357.9 62.7 %all-gather.7.cloned.1.call-done = f32[128,64,128]{2,1,0:T(8,128)} async-done(((f32[8,64,128]{2,1,0:T(8,128)}), f32[128,64,128]{2,1,0:T(8,128)}) %all-gather.7.cloned.1.call-update) | async-done | bytes 4194320 | tf_op jit(solution)/shard_map/all_gather | solution.py:246
  428.8 6.5 %fusion.89 = f32[16]{0:T(128)S(1)} fusion(f32[65536,1]{0,1:T(1,128)S(1)} %bitcast.330, f32[2,8,512,128]{3,2,1,0:T(8,128)S(1)} %bitcast.324), kind=kOutput, calls=%fused_computation.120 | convolution fusion | flops 12582928 | bytes 4456512 | tf_op jit(solution)/shard_map/ik,jk->ij/dot_general | solution.py:254
  439.2 6.8 %fusion.88 = f32[16]{0:T(128)S(1)} fusion(f32[16,65536]{1,0:T(8,128)} %reshape.422, f32[65536,1]{0,1:T(1,128)S(1)} %bitcast.331), kind=kOutput, calls=%fused_computation.119 | convolution fusion | flops 12582928 | bytes 4456512 | tf_op jit(solution)/shard_map/ik,jk->ij/dot_general | solution.py:253
  446.7 13.9 %all-to-all-start.3 = ((f32[8,1,32]{2,1,0:T(1,128)}), f32[8,1,32]{2,1,0:T(1,128)S(1)}, u32[]{:S(2)}, u32[]{:S(2)}) async-start(f32[8,1,32]{2,1,0:T(1,128)} %broadcast_in_dim.180), calls=%async_computation.3 | async-start | bytes 8192 | tf_op jit(solution)/shard_map/all_to_all | solution.py:15
  465.3 21.5 %all-gather.1 = f32[16,1,32]{2,1,0:T(1,128)S(1)} all-gather(f32[1,1,32]{2,1,0:T(1,128)S(1)} %maximum_bitcast_fusion.2), channel_id=1, replica_groups=mesh['kgrp'=2,'band'=16,'fft'=8] {'band'}, dimensions={0}, use_global_device_ids=true | all-gather | bytes 2176 | tf_op jit(solution)/shard_map/all_gather | solution.py:56
  487.0 31.5 %while.52 = (s32[]{:T(128)}, f32[16,16]{1,0:T(8,128)S(1)}, f32[16,16]{1,0:T(8,128)S(1)}, f32[16,16]{0,1:T(8,128)S(1)}, f32[16,16]{0,1:T(8,128)S(1)}, /*index=5*/s32[]{:T(128)}, s32[]{:T(128)}) while((s32[]{:T(128)}, f32[16,16]{1,0:T(8,128)S(1)}, f32[16,16]{1,0:T(8,128)S(1)}, f32[16,16]{0,1:T(8,128)S(1)}, ...), condition=%wide.region_5.6_spmd.clone.clone, body=%wide.region_4.5_spmd.clone.clone.sunk | while | flops 13523 | bytes 48799 | solution.py:185
  518.5 40.5 %while.51 = (s32[]{:T(128)}, f32[16,16]{1,0:T(8,128)S(1)}, f32[16,16]{1,0:T(8,128)S(1)}, f32[16,16]{1,0:T(8,128)S(1)}, f32[16,16]{1,0:T(8,128)S(1)}, /*index=5*/s32[]{:T(128)}, s32[]{:T(128)}) while((s32[]{:T(128)}, f32[16,16]{1,0:T(8,128)S(1)}, f32[16,16]{1,0:T(8,128)S(1)}, f32[16,16]{1,0:T(8,128)S(1)}, f32[16,16]{1,0:T(8,128)S(1)}, ...), condition=%wide.region_7.8_spmd.clone, body=%wide.region_6.7_spmd.clone.sunk | while | flops 14483 | bytes 42011 | solution.py:207
  559.0 6.6 %fusion.79 = f32[1,65536]{1,0:T(1,128)S(1)} fusion(f32[2,8,512,128]{3,2,1,0:T(8,128)} %bitcast.325, f32[16,16]{1,0:T(8,128)S(1)} %get-tuple-element.479, s32[]{:T(128)S(6)} %select_n.229), kind=kOutput, calls=%fused_computation.109 | convolution fusion | flops 12582912 | bytes 4456964 | tf_op jit(solution)/shard_map/dot_general | solution.py:261
  (336 shorter events, 149.8 us)
Async XLA Ops:
  7.2 155.2 %copy-start = (f32[8,3]{0,1:T(4,128)S(1)}, f32[8,3]{0,1:T(4,128)}, u32[]{:S(2)}) copy-start(f32[8,3]{0,1:T(4,128)} %param.12) | copy-start | bytes 292
  7.2 84.5 %all-gather.5.cloned.1.call-start = ((), (), s32[]{:S(2)}) async-start(), calls=%async_computation.4 | async-start | bytes 4456448 | tf_op jit(solution)/shard_map/all_gather | solution.py:222
  8.0 146.6 %copy-start.5 = (f32[1,8,64,128]{3,2,1,0:T(8,128)S(1)}, f32[1,8,64,128]{3,2,1,0:T(8,128)}, u32[]{:S(2)}) copy-start(f32[1,8,64,128]{3,2,1,0:T(8,128)} %param.10) | copy-start | bytes 786436
  154.6 6.8 %copy-start.7 = (s32[16]{0:T(128)S(1)}, s32[16]{0:T(128)}, u32[]{:S(2)}) copy-start(s32[16]{0:T(128)} %param.13) | copy-start | bytes 196
  156.2 30.9 %all-to-all-start.1 = ((f32[8,1,8,64,128]{4,3,2,1,0:T(8,128)}), f32[8,1,8,64,128]{4,3,2,1,0:T(8,128)S(1)}, u32[]{:S(2)}, u32[]{:S(2)}) async-start(f32[8,1,8,64,128]{4,3,2,1,0:T(8,128)} %broadcast_in_dim.178), calls=%async_computation.1 | async-start | bytes 4194304 | tf_op jit(solution)/shard_map/all_to_all | solution.py:15
  160.8 259.8 %all-gather.7.cloned.1.call-start = ((), (), s32[]{:S(2)}) async-start(), calls=%async_computation.5 | async-start | bytes 4456448 | tf_op jit(solution)/shard_map/all_gather | solution.py:246
  250.3 6.7 %copy-start.2 = (f32[2,64,64,128]{3,2,1,0:T(8,128)S(1)}, f32[2,64,64,128]{3,2,1,0:T(8,128)}, u32[]{:S(2)}) copy-start(f32[2,64,64,128]{3,2,1,0:T(8,128)} %get-tuple-element.871) | copy-start | bytes 12582916 | tf_op jit(solution)/shard_map/while
  311.5 6.7 %copy-start.2 = (f32[2,64,64,128]{3,2,1,0:T(8,128)S(1)}, f32[2,64,64,128]{3,2,1,0:T(8,128)}, u32[]{:S(2)}) copy-start(f32[2,64,64,128]{3,2,1,0:T(8,128)} %get-tuple-element.871) | copy-start | bytes 12582916 | tf_op jit(solution)/shard_map/while
  425.6 3.2 copy-start.6
  426.7 2.0 copy-start.3
  446.7 18.5 %all-to-all-start.3 = ((f32[8,1,32]{2,1,0:T(1,128)}), f32[8,1,32]{2,1,0:T(1,128)S(1)}, u32[]{:S(2)}, u32[]{:S(2)}) async-start(f32[8,1,32]{2,1,0:T(1,128)} %broadcast_in_dim.180), calls=%async_computation.3 | async-start | bytes 8192 | tf_op jit(solution)/shard_map/all_to_all | solution.py:15
  559.0 6.6 %copy-start.4 = (f32[16,65536]{1,0:T(8,128)S(1)}, f32[16,65536]{1,0:T(8,128)}, u32[]{:S(2)}) copy-start(f32[16,65536]{1,0:T(8,128)} %reshape.422) | copy-start | bytes 12582916
  559.0 9.4 %copy-start.1 = (f32[8,3]{0,1:T(4,128)S(1)}, f32[8,3]{0,1:T(4,128)}, u32[]{:S(2)}) copy-start(f32[8,3]{0,1:T(4,128)} %param.12) | copy-start | bytes 292
Sparse Core Ops, SparseCore 0:
  9.8 81.8 all-gather.4
  358.0 62.5 all-gather.6
where the time goes:
time: 585 us; the launch traced here: 575 us
  waiting for transfers between devices  172 us (29%)
  matrix products  132 us (23%)
  blocking collectives  115 us (20%)
  local copies, waits for them, and re-layouts  58.1 us (10%)
  other arithmetic  38.3 us (7%)
  loops' own time  28 us (5%)
  starting transfers between devices  18.6 us (3%)
  between operations  14.4 us (2%)
    all_gather x1, waiting for transfers between devices, body(): every_slab = lax.all_gather(partners, 'band', axis=0, tiled=True)  83.7 us
    all_to_all x1, blocking collectives, body(): lax.all_to_all(every_slab, 'fft', split_axis=0, concat_axis=1, tiled=True)  62.9 us
    all_gather x1, waiting for transfers between devices, body(): every_pot = lax.all_gather(potential, 'band', axis=0, tiled=True)  62.7 us
    all_to_all x1, blocking collectives, summed_on_arrival(): lax.all_to_all(pieces, axis, split_axis=0, concat_axis=0, tiled=True)  30.6 us
    dot_general x4, matrix products, along_last(): return jnp.dot(flat, table, precision=HIGHEST).reshape(shape)  26.5 us
    all_to_all x2, waiting for transfers between devices, copy_for_each(): lax.all_to_all(jnp.broadcast_to(x[None], (peers, *x.shape)), axis, 0, 0,...  24.4 us
    another operation x4, local copies, waits for them, and re-layouts  24.3 us
    dot_general x4, matrix products, along_axis(): result = jnp.einsum('kcnd,pnbdz->pkbcz', table, split, precision=HIGHEST)  22.9 us
  transfers between devices with their start and end apart: 4, of which 4 were waited for; matrix products, arithmetic and copies ran while one was open for 1% of the time, Pallas kernels for 0%

commit v1 on v0

v1 whole, which is shorter than its diff:
```python
import math

import jax
import jax.numpy as jnp
import numpy as np
from jax import lax
from jax.experimental import pallas as pl
from jax.experimental.pallas import tpu as pltpu
from jax.sharding import PartitionSpec as P

SCREEN_SQUARE = 0.25
FOUR_PI = 4.0 * math.pi
MESH = pl.DeviceIdType.MESH
PAD = 8
BF = jnp.bfloat16
F32 = jnp.float32


def split_table(table):
    high = np.asarray(table, np.float64).astype(jnp.bfloat16)
    low = (np.asarray(table, np.float64) - high.astype(np.float64)).astype(jnp.bfloat16)
    return high, low


def dft(extent):
    k = np.arange(extent)
    angle = 2.0 * np.pi * ((k[:, None] * k[None, :]) % extent) / extent
    return np.cos(angle), np.sin(angle)


def last_table(extent, sign):
    cosine, sine = dft(extent)
    sine = sign * sine
    table = np.block([[cosine, sine], [-sine, cosine]])
    high, low = split_table(table)
    both = np.concatenate([high, low], axis=1)
    return np.concatenate([both, both], axis=0)


def left_table(extent, sign):
    cosine, sine = dft(extent)
    table = np.concatenate([cosine, -sign * sine], axis=1)
    high, low = split_table(table)
    return np.concatenate(
        [np.concatenate([high, high], axis=1), np.concatenate([low, low], axis=1)], axis=0
    )


def halves(v):
    high = v.astype(BF)
    low = (v - high.astype(F32)).astype(BF)
    return high, low


def swapped(v):
    return pltpu.roll(v, v.shape[-1] // 2, 1)


def lane_sign(shape, first, second):
    lane = lax.broadcasted_iota(jnp.int32, shape, len(shape) - 1)
    return jnp.where(lane < shape[-1] // 2, first, second).astype(F32)


def turned(v):
    return swapped(v) * lane_sign((1, v.shape[-1]), 1.0, -1.0)


def mm(a, b):
    return jnp.dot(a, b, preferred_element_type=F32)


def along_last(v, table):
    high, low = halves(v)
    width = v.shape[-1]
    both = mm(jnp.concatenate([high, low], axis=1), table)
    return both[:, :width] + both[:, width:]


def left_column(v):
    high, low = halves(v)
    thigh, tlow = halves(turned(v))
    return jnp.concatenate([high, thigh, low, tlow], axis=0)


def along_left(blocks, table):
    rows = table.shape[0] // 2
    columns = jnp.concatenate([left_column(v) for v in blocks], axis=1)
    both = mm(table, columns)
    out = both[:rows] + both[rows:]
    width = blocks[0].shape[-1]
    return [out[:, k * width : (k + 1) * width] for k in range(len(blocks))]


def kernel(
    nb, nf, n, p_hbm, u_hbm, zf_ref, zi_ref, lf_ref, li_ref, tab_ref, idx_ref,
    pot_ref, proj_ref,
    pfull, ufull, dbuf, vbuf, d2d, hops, usub, vsub, psub, mine, mrow, mcol, mall,
    perm_s, perm_r, loc, agz_s, agz_r, agx_s, agx_r, du_s, du_r, dv_s, dv_r, rs_s, rs_r,
    au_s, au_r, av_s, av_r, ap_s, ap_r, mf_s, mf_r, mb_s, mb_r,
):
    slab = p_hbm.shape[0]
    half = slab // 2
    planes = slab // n
    width = p_hbm.shape[1]
    nx = nf // 2
    part = slab // nb
    pitch = n + PAD
    b = lax.axis_index("band")
    f = lax.axis_index("fft")
    x, c = f // 2, f % 2
    mate = f + 1 - 2 * c
    right, left = (b + 1) % nb, (b + nb - 1) % nb
    fright, fleft = (f + 2) % nf, (f + nf - 2) % nf
    slot = (b - f + nf // 2 + nb) % nb
    to_band, to_fft, to_slot = (b - nf // 2 + f + nb) % nb, b % nf, (b // nf) * nf + f
    from_band, from_fft = f + nf * (slot // nf), slot % nf
    alone = jnp.logical_and(to_band == b, to_fft == f)

    def rows(start, count):
        return pl.ds(pl.multiple_of(start, 8), count)

    def rc(src, dst, ssem, rsem, **dev):
        return pltpu.make_async_remote_copy(
            src_ref=src, dst_ref=dst, send_sem=ssem, recv_sem=rsem, device_id=dev,
            device_id_type=MESH,
        )

    barrier = pltpu.get_barrier_semaphore()

    def greet(**dev):
        pl.semaphore_signal(barrier, inc=1, device_id=dev, device_id_type=MESH)

    @pl.loop(1, nb)
    def _(d):
        greet(band=(b + d) % nb)

    @pl.loop(1, nf)
    def _(d):
        greet(fft=(f + d) % nf)

    @pl.when(jnp.logical_not(alone))
    def _():
        greet(band=to_band, fft=to_fft)
        greet(band=from_band, fft=from_fft)

    u_local = pltpu.make_async_copy(u_hbm, ufull.at[rows(f * slab, slab)], loc.at[0])
    u_local.start()
    pl.semaphore_wait(barrier, nb - 1 + nf - 1 + jnp.where(alone, 0, 2))

    def perm(h):
        return rc(
            p_hbm.at[rows(h * half, half)], pfull.at[rows(to_slot * slab + h * half, half)],
            perm_s.at[h], perm_r.at[h], band=to_band, fft=to_fft,
        )

    def perm_here(h):
        return rc(
            p_hbm.at[rows(h * half, half)], pfull.at[rows(slot * slab + h * half, half)],
            perm_s.at[h], perm_r.at[h], band=from_band, fft=from_fft,
        )

    def perm_local(h):
        return pltpu.make_async_copy(
            p_hbm.at[rows(h * half, half)], pfull.at[rows(slot * slab + h * half, half)],
            loc.at[1 + h],
        )

    @pl.when(jnp.logical_not(alone))
    def _():
        perm(0).start()
        perm(1).start()

    @pl.when(alone)
    def _():
        perm_local(0).start()
        perm_local(1).start()

    def slab_of(dx, core):
        return 2 * ((x + dx) % nx) + core

    def agx1(h, way):
        return rc(
            u_hbm.at[rows(h * half, half)], ufull.at[rows(f * slab + h * half, half)],
            agx_s.at[0, h, way], agx_r.at[0, h, way], fft=fright if way == 0 else fleft,
        )

    def agx1_here(h, way):
        owner = slab_of(nx - 1 if way == 0 else 1, c)
        return rc(
            u_hbm.at[rows(h * half, half)], ufull.at[rows(owner * slab + h * half, half)],
            agx_s.at[0, h, way], agx_r.at[0, h, way], fft=fright if way == 0 else fleft,
        )

    def agx2(way):
        owner = slab_of(nx - 1 if way == 0 else 1, c)
        piece = ufull.at[rows(owner * slab + way * half, half)]
        return rc(
            piece, piece, agx_s.at[1, 0, way], agx_r.at[1, 0, way],
            fft=fright if way == 0 else fleft,
        )

    def agx2_here(way):
        piece = ufull.at[rows(slab_of(2, c) * slab + way * half, half)]
        return rc(
            piece, piece, agx_s.at[1, 0, way], agx_r.at[1, 0, way],
            fft=fright if way == 0 else fleft,
        )

    def du(k, core):
        piece = ufull.at[rows(slab_of((0, nx - 1, 1, 2)[k], core) * slab, slab)]
        src = u_hbm if (k == 0) else piece
        return rc(src, piece, du_s.at[k], du_r.at[k], fft=mate)

    for way in (0, 1):
        agx1(way, way).start()
    for way in (0, 1):
        agx1(1 - way, way).start()
    du(0, c).start()

    def agz(s, h, way):
        owner = (slot - (s - 1) + nb) % nb if way == 0 else (slot + (s - 1)) % nb
        piece = pfull.at[rows(owner * slab + h * half, half)]
        return rc(
            piece, piece, agz_s.at[s, h, way], agz_r.at[s, h, way],
            band=right if way == 0 else left,
        )

    def agz_here(s, h, way):
        owner = (slot - s + nb) % nb if way == 0 else (slot + s) % nb
        piece = pfull.at[rows(owner * slab + h * half, half)]
        return rc(
            piece, piece, agz_s.at[s, h, way], agz_r.at[s, h, way],
            band=right if way == 0 else left,
        )

    for h in (0, 1):
        @pl.when(jnp.logical_not(alone))
        def _():
            perm_here(h).wait_recv()

        @pl.when(alone)
        def _():
            perm_local(h).wait()

        for way in (0, 1):
            agz(1, h, way).start()

    for way in (0, 1):
        agx1_here(way, way).wait_recv()
        agx2(way).start()
    for way in (0, 1):
        agx1_here(1 - way, way).wait_recv()
        du(1 + way, c).start()

    for h in (0, 1):
        for way in (0, 1):
            agz_here(1, h, way).wait_recv()
            agz(2, h, way).start()

    for way in (0, 1):
        agx2_here(way).wait_recv()
    du(3, c).start()
    u_local.wait()
    for k in range(4):
        du(k, 1 - c).wait_recv()

    first_lanes = lax.broadcasted_iota(jnp.int32, (1, width), 1) < width // 2
    batch = 4

    def forward_planes(owner, k):
        a, s = owner // nf, owner % nf
        p = pfull[rows(owner * slab + k * batch * n, batch * n), :]
        u = ufull[rows(s * slab + k * batch * n, batch * n), :]
        ps, us = swapped(p), swapped(u)
        real = jnp.where(first_lanes, p, ps)
        imag = jnp.where(first_lanes, ps, -p)
        rho = real * u + imag * us
        spec = along_last(rho, zf_ref[...])
        base = (a * n + s * planes + k * batch) * pitch
        for q in range(0, batch, 2):
            outs = along_left(
                [spec[q * n : (q + 1) * n], spec[(q + 1) * n : (q + 2) * n]], lf_ref[...]
            )
            for e in (0, 1):
                dbuf[rows(base + (q + e) * pitch, n), :] = outs[e]

    last = nb // 2

    @pl.loop(3, last + 3)
    def _(s):
        @pl.when(s < last)
        def _():
            for h in (0, 1):
                for way in (0, 1):
                    agz_here(s - 1, h, way).wait_recv()
                    agz(s, h, way).start()

        @pl.when(s == last)
        def _():
            for h in (0, 1):
                for way in (0, 1):
                    agz_here(s - 1, h, way).wait_recv()
                    if h == way:
                        agz(s, h, way).start()

        @pl.when(s == last + 1)
        def _():
            for way in (0, 1):
                agz_here(last, way, way).wait_recv()

        end = s == last + 2
        low = (slot - jnp.where(end, 0, s - 2) + nb) % nb
        high = (slot + jnp.where(end, last, s - 2)) % nb

        @pl.loop(0, 2 * (planes // batch))
        def _(k):
            owner = jnp.where(k < planes // batch, low, high)
            forward_planes(owner, k % (planes // batch))

    def a2a(src_of, dst, ssem, rsem, d):
        to = (b + d) % nb
        return rc(src_of(to), dst.at[rows(b * part, part)], ssem.at[d], rsem.at[d], band=to)

    def a2a_here(src_of, dst, ssem, rsem, d):
        to = (b + d) % nb
        source = (b - d + nb) % nb
        return rc(src_of(to), dst.at[rows(source * part, part)], ssem.at[d], rsem.at[d], band=to)

    au = (lambda t: u_hbm.at[rows(t * part, part)], usub, au_s, au_r)

    @pl.loop(1, nb)
    def _(d):
        a2a(*au, d).start()

    u_mine = pltpu.make_async_copy(
        u_hbm.at[rows(b * part, part)], usub.at[rows(b * part, part)], loc.at[3]
    )
    u_mine.start()

    freq = lax.broadcasted_iota(jnp.int32, (n, width), 0)
    freq = jnp.where(freq < n // 2, freq, freq - n).astype(F32)
    lane = lax.broadcasted_iota(jnp.int32, (n, width), 1) % n
    lane = jnp.where(lane < n // 2, lane, lane - n).astype(F32)
    shift = []
    for a in (0, 1):
        row = idx_ref[f + nf * a]
        shift.append([tab_ref[row, e] for e in range(3)])
    for a in (0, 1):
        fx = freq + shift[a][0]
        fz = lane + shift[a][2]
        hops[rows(a * n, n), :] = fx * fx + fz * fz + SCREEN_SQUARE
    scale = FOUR_PI / n**3
    per = 2

    @pl.loop(0, n // per)
    def _(k):
        for a in (0, 1):
            ys = [k * per + e for e in range(per)]
            take = [pl.ds(a * n * pitch + y, n, stride=pitch) for y in ys]
            spectra = along_left([dbuf[t, :] for t in take], lf_ref[...])
            base = hops[pl.ds(a * n, n), :]
            screened = []
            for y, spectrum in zip(ys, spectra):
                fy = jnp.where(y < n // 2, y, y - n).astype(F32) + shift[a][1]
                screened.append(spectrum * (scale / (base + fy * fy)))
            fields = along_left(screened, li_ref[...])
            for t, field in zip(take, fields):
                dbuf[t, :] = field

    def dv(k):
        src = vbuf.at[rows(slab_at(k, 1 - c) * slab, slab)]
        return rc(src, d2d.at[rows(k * slab, slab)], dv_s.at[k], dv_r.at[k], fft=mate)

    def slab_at(k, core):
        dx = jnp.where(k == 0, 2, jnp.where(k == 1, 1, jnp.where(k == 2, nx - 1, 0)))
        return slab_of(dx, core)

    def hop(k, src, way):
        return rc(
            src, hops.at[rows(2 * n + k * half, half)], rs_s.at[k], rs_r.at[k],
            fft=fright if way == 0 else fleft,
        )

    def piece(dx, h):
        return vbuf.at[rows(slab_of(dx, c) * slab + h * half, half)]

    def hop_of(k):
        way = k % 2
        toward = 1 if way == 0 else nx - 1
        if k < 2:
            return hop(k, piece(2, way), way)
        if k < 4:
            return hop(k, piece(toward, 1 - way), way)
        return hop(k, piece(toward, way), way)

    def inverse_planes(s, k):
        total = None
        for a in (0, 1):
            base = (a * n + s * planes + k * batch) * pitch
            fields = []
            for q in range(0, batch, 2):
                fields += along_left(
                    [dbuf[rows(base + (q + e) * pitch, n), :] for e in (0, 1)], li_ref[...]
                )
            field = along_last(jnp.concatenate(fields, axis=0), zi_ref[...])
            p = pfull[rows((a * nf + s) * slab + k * batch * n, batch * n), :]
            ps = swapped(p)
            real = jnp.where(first_lanes, p, ps)
            imag = jnp.where(first_lanes, -ps, p)
            term = real * field + imag * swapped(field)
            total = term if total is None else total + term
        vbuf[rows(s * slab + k * batch * n, batch * n), :] = total

    @pl.loop(0, 2 * nx)
    def _(i):
        own = i >= nx
        k = i % nx
        s = slab_at(k, jnp.where(own, c, 1 - c))

        @pl.loop(0, planes // batch)
        def _(q):
            inverse_planes(s, q)

        @pl.when(jnp.logical_not(own))
        def _():
            dv(k).start()

        @pl.when(own)
        def _():
            dv(k).wait_recv()
            vbuf[rows(s * slab, slab), :] += d2d[rows(k * slab, slab), :]

        @pl.when(i == nx)
        def _():
            hop_of(0).start()
            hop_of(1).start()

        @pl.when(i == nx + 1)
        def _():
            hop_of(2).start()

        @pl.when(i == nx + 2)
        def _():
            hop_of(3).start()

    def arrived(k):
        return hops[rows(2 * n + k * half, half), :]

    for way in (0, 1):
        hop_of(way).wait_recv()
        toward = slab_of(1 if way == 0 else nx - 1, c)
        vbuf[rows(toward * slab + way * half, half), :] += arrived(way)
        hop_of(4 + way).start()
    for k in (2, 3, 4, 5):
        hop_of(k).wait_recv()
    pot_ref[0:half, :] = vbuf[rows(f * slab, half), :] + arrived(3) + arrived(4)
    pot_ref[half:slab, :] = vbuf[rows(f * slab + half, half), :] + arrived(2) + arrived(5)

    av = (lambda t: pot_ref.at[rows(t * part, part)], vsub, av_s, av_r)

    @pl.loop(1, nb)
    def _(d):
        a2a(*av, d).start()

    vsub[rows(b * part, part), :] = pot_ref[rows(b * part, part), :]
    u_mine.wait()

    @pl.loop(1, nb)
    def _(d):
        a2a_here(*au, d).wait_recv()

    @pl.loop(1, nb)
    def _(d):
        a2a_here(*av, d).wait_recv()

    group = 4
    acc = jnp.zeros((2 * nb, 4 * nb), F32)
    for g in range(0, part, group):
        us = [usub[pl.ds(g + e, nb, stride=part), :] for e in range(group)]
        vs = [vsub[pl.ds(g + e, nb, stride=part), :] for e in range(group)]
        uh, ul = halves(jnp.concatenate(us, axis=1))
        vh, vl = halves(jnp.concatenate(vs, axis=1))
        th, tl = halves(jnp.concatenate([turned(v) for v in vs], axis=1))
        acc += lax.dot_general(
            jnp.concatenate([uh, ul], axis=0), jnp.concatenate([vh, th, vl, tl], axis=0),
            (((1,), (1,)), ((), ())), preferred_element_type=F32,
        )
    acc = acc[:nb] + acc[nb:]
    acc = (acc[:, : 2 * nb] + acc[:, 2 * nb :]) * (1.0 / n**3)
    mine[...] = jnp.concatenate([acc, jnp.zeros((nb, width - 2 * nb), F32)], axis=1)

    def mf(d, here=False):
        to = (f + d) % nf
        source = (f - d + nf) % nf
        at = source if here else f
        return rc(mine, mrow.at[rows(at * nb, nb)], mf_s.at[d], mf_r.at[d], fft=to)

    def mb(d, here=False):
        to = (b + d) % nb
        source = (b - d + nb) % nb
        at = source if here else b
        return rc(mcol, mall.at[rows(at * nb, nb)], mb_s.at[d], mb_r.at[d], band=to)

    for d in range(1, nf):
        mf(d).start()
    mrow[rows(f * nb, nb), :] = mine[...]
    for d in range(1, nf):
        mf(d, True).wait_recv()
    total = mrow[0:nb, :]
    for k in range(1, nf):
        total += mrow[k * nb : (k + 1) * nb, :]
    mcol[...] = total

    @pl.loop(1, nb)
    def _(d):
        mb(d).start()

    mall[rows(b * nb, nb), :] = mcol[...]

    @pl.loop(1, nb)
    def _(d):
        mb(d, True).wait_recv()

    total = mall[0:nb, :]
    for k in range(1, nb):
        total += mall[k * nb : (k + 1) * nb, :]

    ri = lax.broadcasted_iota(jnp.int32, (nb, nb), 0)
    ci = lax.broadcasted_iota(jnp.int32, (nb, nb), 1)
    eye = (ri == ci).astype(F32)

    def flipped(m):
        return lax.dot_general(
            eye, m, (((1,), (1,)), ((), ())), precision=lax.Precision.HIGHEST,
            preferred_element_type=F32,
        )

    mre, mim = total[:, :nb], total[:, nb : 2 * nb]
    hre = jnp.where(ri >= ci, mre, flipped(mre))
    him = jnp.where(ri > ci, mim, jnp.where(ri < ci, -flipped(mim), 0.0))
    zero = jnp.zeros((nb, nb), F32)
    work = jnp.concatenate([hre, him, eye, zero], axis=1)
    other = jnp.concatenate([-him, hre, zero, eye], axis=1)
    row_at = lax.broadcasted_iota(jnp.int32, (nb, 1), 0)
    for k in range(nb):
        pivot = work[k : k + 1, k : k + 1]
        cre = jnp.where(row_at > k, work[:, k : k + 1], 0.0) / pivot
        cim = jnp.where(row_at > k, work[:, nb + k : nb + k + 1], 0.0) / pivot
        row, rot = work[k : k + 1, :], other[k : k + 1, :]
        work = work - (cre * row + cim * rot)
        other = other - (cre * rot - cim * row)
    pivots = jnp.sum(work[:, :nb] * eye, axis=1, keepdims=True)
    coef = work[:, 2 * nb : 4 * nb] / jnp.sqrt(pivots)
    ch, cl = halves(coef)
    coef = jnp.concatenate(
        [jnp.concatenate([ch, ch], axis=1), jnp.concatenate([cl, cl], axis=1)], axis=0
    )

    for g in range(0, part, group):
        vs = [vsub[pl.ds(g + e, nb, stride=part), :] for e in range(group)]
        cols = jnp.concatenate([left_column(v) for v in vs], axis=1)
        both = mm(coef, cols)
        out = both[:nb] + both[nb:]
        for e in range(group):
            psub[pl.ds(g + e, nb, stride=part), :] = out[:, e * width : (e + 1) * width]

    ap = (lambda t: psub.at[rows(t * part, part)], proj_ref, ap_s, ap_r)

    @pl.loop(1, nb)
    def _(d):
        a2a(*ap, d).start()

    proj_ref[rows(b * part, part), :] = psub[rows(b * part, part), :]

    @pl.when(jnp.logical_not(alone))
    def _():
        perm(0).wait_send()
        perm(1).wait_send()

    for way in (0, 1):
        for h in (0, 1):
            agx1(h, way).wait_send()
        agx2(way).wait_send()
    for k in range(4):
        du(k, c).wait_send()

    @pl.loop(1, last)
    def _(s):
        for h in (0, 1):
            for way in (0, 1):
                agz(s, h, way).wait_send()

    for way in (0, 1):
        agz(last, way, way).wait_send()

    @pl.loop(0, nx)
    def _(k):
        dv(k).wait_send()

    for k in range(6):
        hop_of(k).wait_send()
    for d in range(1, nf):
        mf(d).wait_send()

    @pl.loop(1, nb)
    def _(d):
        a2a(*au, d).wait_send()
        a2a(*av, d).wait_send()
        mb(d).wait_send()
        a2a(*ap, d).wait_send()

    @pl.loop(1, nb)
    def _(d):
        a2a_here(*ap, d).wait_recv()


def body(mesh, orbitals, partners, shift_table, shift_index):
    nb, nf = mesh.shape["band"], mesh.shape["fft"]
    n = orbitals.shape[2]
    width = orbitals.shape[3]
    slab = orbitals.shape[0] * orbitals.shape[1] * n
    part = slab // nb
    assert nb == 2 * nf and nf == 8 and orbitals.shape[0] == 1

    def call(p, u, *rest):
        any_spec = pl.BlockSpec(memory_space=pl.ANY)
        vmem = pl.BlockSpec(memory_space=pltpu.VMEM)
        smem = pl.BlockSpec(memory_space=pltpu.SMEM)
        dma = pltpu.SemaphoreType.DMA
        out = jax.ShapeDtypeStruct((slab, width), F32)
        half = slab // 2
        return pl.pallas_call(
            lambda *refs: kernel(nb, nf, n, *refs),
            out_shape=(out, out),
            in_specs=[any_spec, any_spec, vmem, vmem, vmem, vmem, smem, smem],
            out_specs=(vmem, vmem),
            scratch_shapes=[
                pltpu.VMEM((nb * slab, width), F32),
                pltpu.VMEM((nf * slab, width), F32),
                pltpu.VMEM((2 * n * (n + PAD), width), F32),
                pltpu.VMEM((nf * slab, width), F32),
                pltpu.VMEM((nf // 2 * slab, width), F32),
                pltpu.VMEM((2 * n + 6 * half, width), F32),
                pltpu.VMEM((slab, width), F32),
                pltpu.VMEM((slab, width), F32),
                pltpu.VMEM((slab, width), F32),
                pltpu.VMEM((nb, width), F32),
                pltpu.VMEM((nf * nb, width), F32),
                pltpu.VMEM((nb, width), F32),
                pltpu.VMEM((nb * nb, width), F32),
                dma((2,)), dma((2,)), dma((4,)),
                dma((nb // 2 + 1, 2, 2)), dma((nb // 2 + 1, 2, 2)),
                dma((2, 2, 2)), dma((2, 2, 2)),
                dma((4,)), dma((4,)), dma((4,)), dma((4,)), dma((6,)), dma((6,)),
                dma((nb,)), dma((nb,)), dma((nb,)), dma((nb,)), dma((nb,)), dma((nb,)),
                dma((nf,)), dma((nf,)), dma((nb,)), dma((nb,)),
            ],
            compiler_params=pltpu.CompilerParams(collective_id=0, has_side_effects=True),
            name="exchange",
        )(p, u, *rest)

    tables = [
        jnp.asarray(t)
        for t in (last_table(n, -1.0), last_table(n, 1.0), left_table(n, -1.0), left_table(n, 1.0))
    ]
    pot, proj = call(
        partners.reshape(slab, width), orbitals.reshape(slab, width), *tables,
        shift_table, shift_index,
    )
    return pot.reshape(orbitals.shape), proj.reshape(orbitals.shape)


def solution(mesh):
    spec = P(("kgrp", "band"), "fft", None, None)
    return jax.shard_map(
        lambda *args: body(mesh, *args), mesh=mesh, in_specs=(spec, spec, P(), P("kgrp")),
        out_specs=(spec, spec), check_vma=False,
    )
```

time: 585 us -> 183 us (0.31); the launches traced: 575 us -> 182 us
  Pallas kernels: 0 us -> 178 us
  waiting for transfers between devices: 172 us -> 0 us
  matrix products: 132 us -> 0 us
  blocking collectives: 115 us -> 0 us
  local copies, waits for them, and re-layouts: 58.1 us -> 3.77 us
  other arithmetic: 38.3 us -> 0 us
  loops' own time: 28 us -> 0 us
  starting transfers between devices: 18.6 us -> 0 us
  between operations: 14.4 us -> 0.66 us
    pallas_call x0 -> x1, Pallas kernels: none -> 178 us  [call(): pl.pallas_call(lambda *refs: kernel(nb, nf, n, *refs), out_shape=(out, ou...]
    all_gather x2 -> x0, waiting for transfers between devices: 146 us -> none  [the longest x1 83.7 us: body(): every_slab = lax.all_gather(partners, 'band', axis=0, tiled=True)]
    dot_general x145 -> x0, matrix products: 132 us -> none  [the longest x4 26.5 us: along_last(): return jnp.dot(flat, table, precision=HIGHEST).reshape(shape)]
    all_to_all x2 -> x0, blocking collectives: 93.5 us -> none  [the longest x1 62.9 us: body(): lax.all_to_all(every_slab, 'fft', split_axis=0, concat_axis=1, tiled=True)]
    another operation x3 -> x0, loops' own time: 28 us -> none  [the longest x1 16.2 us: body(): lax.fori_loop(0, own_count, one_partner, jnp.zeros(full_orbitals.shape, j...]
    all_to_all x2 -> x0, waiting for transfers between devices: 24.4 us -> none  [copy_for_each(): lax.all_to_all(jnp.broadcast_to(x[None], (peers, *x.shape)), axis, 0, 0,...]
    another operation x4 -> x0, local copies, waits for them, and re-layouts: 24.3 us -> none
    all_gather x1 -> x0, blocking collectives: 21.5 us -> none  [in_one_piece(): out = lax.all_gather(both, axis, axis=dim, tiled=True)]
  transfers between devices with their start and end apart: 4 -> 0, of which waited for: 4 -> 0; matrix products, arithmetic and copies ran while one was open for 1% -> 0% of each run, Pallas kernels for 0% -> 0%
where the time goes in v1:
time: 183 us; the launch traced here: 182 us
  Pallas kernels  178 us (97%)
  local copies, waits for them, and re-layouts  3.77 us (2%)
    pallas_call x1, Pallas kernels, call(): pl.pallas_call(lambda *refs: kernel(nb, nf, n, *refs), out_shape=(out, ou...  178 us
    unnamed x7, local copies, waits for them, and re-layouts  3.77 us

profile of v1, /device:TPU:33, one launch (start us, length us, event | category | flops | bytes accessed | tf_op | source)
XLA Modules:
  0.0 182.4 jit_solution(6252323250594413847)
XLA Ops:
  0.6 0.0 copy-start.1
  0.6 0.7 copy-done.1
  1.3 0.7 copy.10.refs_6_
  2.0 178.0 %exchange.1 = (f32[512,128]{1,0:T(8,128)}, f32[512,128]{1,0:T(8,128)}) custom-call(f32[512,128]{1,0:T(8,128)} %bitcast.4, f32[512,128]{1,0:T(8,128)} %bitcast.5, bf16[256,256]{1,0:T(8,128)(2,1)} %constant.8.clone.refs_2_, bf16[256,256]{1,0:T(8,128)(2,1)} %constant.9.clone.refs_3_, bf16[128,256]{1,0:T(8,128)(2,1)} %constant.10.clone.refs_4_, ...), custom_call_target="tpu_custom_call" | custom-call | tf_op jit(solution)/shard_map/exchange/pallas_call | solution.py:632
  180.0 0.0 copy-start
  180.0 1.7 copy.13
  181.7 0.0 copy-done
  181.7 0.7 copy.14
Async XLA Ops:
  0.6 0.7 copy-start.1
  180.0 1.7 copy-start

commit v2 on v1

--- a/solution.py
+++ b/solution.py
@@ -11,6 +11,7 @@
 SCREEN_SQUARE = 0.25
 FOUR_PI = 4.0 * math.pi
 MESH = pl.DeviceIdType.MESH
+SPREAD = 5
 PAD = 8
 BF = jnp.bfloat16
 F32 = jnp.float32
@@ -100,6 +101,8 @@
 ):
     slab = p_hbm.shape[0]
     half = slab // 2
+    quarters = 4
+    quarter = slab // quarters
     planes = slab // n
     width = p_hbm.shape[1]
     nx = nf // 2
@@ -111,10 +114,17 @@
     mate = f + 1 - 2 * c
     right, left = (b + 1) % nb, (b + nb - 1) % nb
     fright, fleft = (f + 2) % nf, (f + nf - 2) % nf
-    slot = (b - f + nf // 2 + nb) % nb
-    to_band, to_fft, to_slot = (b - nf // 2 + f + nb) % nb, b % nf, (b // nf) * nf + f
-    from_band, from_fft = f + nf * (slot // nf), slot % nf
+    lead = x + nx * c
+    slot = (b - lead + nf // 2 + nb) % nb
+    to_band = (b - nf // 2 + (SPREAD * f) % nf + nb) % nb
+    to_fft = 2 * (b % nx) + (b // nx) % 2
+    to_slot = (b // nf) * nf + f
+    from_fft = (SPREAD * slot) % nf
+    from_band = lead + nf * (slot // nf)
     alone = jnp.logical_and(to_band == b, to_fft == f)
+
+    def farthest_first(i, count):
+        return count // 2 + jnp.where(i % 2 == 0, i // 2, -(i // 2))
 
     def rows(start, count):
         return pl.ds(pl.multiple_of(start, 8), count)
@@ -130,13 +140,11 @@
     def greet(**dev):
         pl.semaphore_signal(barrier, inc=1, device_id=dev, device_id_type=MESH)
 
-    @pl.loop(1, nb)
-    def _(d):
-        greet(band=(b + d) % nb)
-
-    @pl.loop(1, nf)
-    def _(d):
-        greet(fft=(f + d) % nf)
+    greet(band=right)
+    greet(band=left)
+    greet(fft=fright)
+    greet(fft=fleft)
+    greet(fft=mate)
 
     @pl.when(jnp.logical_not(alone))
     def _():
@@ -145,35 +153,40 @@
 
     u_local = pltpu.make_async_copy(u_hbm, ufull.at[rows(f * slab, slab)], loc.at[0])
     u_local.start()
-    pl.semaphore_wait(barrier, nb - 1 + nf - 1 + jnp.where(alone, 0, 2))
-
-    def perm(h):
-        return rc(
-            p_hbm.at[rows(h * half, half)], pfull.at[rows(to_slot * slab + h * half, half)],
-            perm_s.at[h], perm_r.at[h], band=to_band, fft=to_fft,
-        )
-
-    def perm_here(h):
-        return rc(
-            p_hbm.at[rows(h * half, half)], pfull.at[rows(slot * slab + h * half, half)],
-            perm_s.at[h], perm_r.at[h], band=from_band, fft=from_fft,
-        )
-
-    def perm_local(h):
+    pl.semaphore_wait(barrier, jnp.where(alone, 5, 7))
+
+    def place(at):
+        return (at // nf) * nf + (SPREAD * at) % nf
+
+    def perm(q):
+        return rc(
+            p_hbm.at[rows(q * quarter, quarter)],
+            pfull.at[rows(to_slot * slab + q * quarter, quarter)],
+            perm_s.at[q], perm_r.at[q], band=to_band, fft=to_fft,
+        )
+
+    def perm_here(q):
+        return rc(
+            p_hbm.at[rows(q * quarter, quarter)],
+            pfull.at[rows(place(slot) * slab + q * quarter, quarter)],
+            perm_s.at[q], perm_r.at[q], band=from_band, fft=from_fft,
+        )
+
+    def perm_local(q):
         return pltpu.make_async_copy(
-            p_hbm.at[rows(h * half, half)], pfull.at[rows(slot * slab + h * half, half)],
-            loc.at[1 + h],
+            p_hbm.at[rows(q * quarter, quarter)],
+            pfull.at[rows(place(slot) * slab + q * quarter, quarter)], loc.at[2 + q],
         )
 
     @pl.when(jnp.logical_not(alone))
     def _():
-        perm(0).start()
-        perm(1).start()
+        for q in range(quarters):
+            perm(q).start()
 
     @pl.when(alone)
     def _():
-        perm_local(0).start()
-        perm_local(1).start()
+        for q in range(quarters):
+            perm_local(q).start()
 
     def slab_of(dx, core):
         return 2 * ((x + dx) % nx) + core
@@ -211,52 +224,56 @@
         src = u_hbm if (k == 0) else piece
         return rc(src, piece, du_s.at[k], du_r.at[k], fft=mate)
 
+    du(0, c).start()
+
+    def agz(s, q, way):
+        owner = (slot - (s - 1) + nb) % nb if way == 0 else (slot + (s - 1)) % nb
+        piece = pfull.at[rows(place(owner) * slab + q * quarter, quarter)]
+        return rc(
+            piece, piece, agz_s.at[s, q, way], agz_r.at[s, q, way],
+            band=right if way == 0 else left,
+        )
+
+    def agz_here(s, q, way):
+        owner = (slot - s + nb) % nb if way == 0 else (slot + s) % nb
+        piece = pfull.at[rows(place(owner) * slab + q * quarter, quarter)]
+        return rc(
+            piece, piece, agz_s.at[s, q, way], agz_r.at[s, q, way],
+            band=right if way == 0 else left,
+        )
+
+    for q in range(quarters):
+        @pl.when(jnp.logical_not(alone))
+        def _():
+            perm_here(q).wait_recv()
+
+        @pl.when(alone)
+        def _():
+            perm_local(q).wait()
+
+        for way in (0, 1):
+            agz(1, q, way).start()
+
     for way in (0, 1):
         agx1(way, way).start()
     for way in (0, 1):
         agx1(1 - way, way).start()
-    du(0, c).start()
-
-    def agz(s, h, way):
-        owner = (slot - (s - 1) + nb) % nb if way == 0 else (slot + (s - 1)) % nb
-        piece = pfull.at[rows(owner * slab + h * half, half)]
-        return rc(
-            piece, piece, agz_s.at[s, h, way], agz_r.at[s, h, way],
-            band=right if way == 0 else left,
-        )
-
-    def agz_here(s, h, way):
-        owner = (slot - s + nb) % nb if way == 0 else (slot + s) % nb
-        piece = pfull.at[rows(owner * slab + h * half, half)]
-        return rc(
-            piece, piece, agz_s.at[s, h, way], agz_r.at[s, h, way],
-            band=right if way == 0 else left,
-        )
-
-    for h in (0, 1):
-        @pl.when(jnp.logical_not(alone))
-        def _():
-            perm_here(h).wait_recv()
-
-        @pl.when(alone)
-        def _():
-            perm_local(h).wait()
-
+
+    def forward(s, q):
         for way in (0, 1):
-            agz(1, h, way).start()
-
+            agz_here(s - 1, q, way).wait_recv()
+            agz(s, q, way).start()
+
+    for q in range(quarters):
+        forward(2, q)
     for way in (0, 1):
         agx1_here(way, way).wait_recv()
         agx2(way).start()
+    for q in range(quarters):
+        forward(3, q)
     for way in (0, 1):
         agx1_here(1 - way, way).wait_recv()
         du(1 + way, c).start()
-
-    for h in (0, 1):
-        for way in (0, 1):
-            agz_here(1, h, way).wait_recv()
-            agz(2, h, way).start()
-
     for way in (0, 1):
         agx2_here(way).wait_recv()
     du(3, c).start()
@@ -286,36 +303,44 @@
 
     last = nb // 2
 
-    @pl.loop(3, last + 3)
-    def _(s):
+    per_slab = planes // batch
+
+    def items_ready(t):
+        ready = per_slab * (2 * (t // quarters + first - 2) + 1)
+        return jnp.minimum(jnp.minimum(2 * (t + 1), ready), nb * per_slab)
+
+    first = 4
+
+    @pl.loop(0, quarters * (last + 2 - first) + 1)
+    def _(t):
+        s, q = first + t // quarters, t % quarters
+
         @pl.when(s < last)
         def _():
-            for h in (0, 1):
-                for way in (0, 1):
-                    agz_here(s - 1, h, way).wait_recv()
-                    agz(s, h, way).start()
+            forward(s, q)
 
         @pl.when(s == last)
         def _():
-            for h in (0, 1):
-                for way in (0, 1):
-                    agz_here(s - 1, h, way).wait_recv()
-                    if h == way:
-                        agz(s, h, way).start()
+            for way in (0, 1):
+                agz_here(s - 1, q, way).wait_recv()
+
+                @pl.when(2 * q // quarters == way)
+                def _():
+                    agz(s, q, way).start()
 
         @pl.when(s == last + 1)
         def _():
             for way in (0, 1):
-                agz_here(last, way, way).wait_recv()
-
-        end = s == last + 2
-        low = (slot - jnp.where(end, 0, s - 2) + nb) % nb
-        high = (slot + jnp.where(end, last, s - 2)) % nb
-
-        @pl.loop(0, 2 * (planes // batch))
-        def _(k):
-            owner = jnp.where(k < planes // batch, low, high)
-            forward_planes(owner, k % (planes // batch))
+                @pl.when(2 * q // quarters == way)
+                def _():
+                    agz_here(last, q, way).wait_recv()
+
+        @pl.loop(jnp.where(t == 0, 0, items_ready(t - 1)), items_ready(t))
+        def _(w):
+            order, k = w // per_slab, w % per_slab
+            far = (order + 1) // 2
+            owner = jnp.where(order % 2 == 1, slot + far, slot - far + nb) % nb
+            forward_planes(place(owner), k)
 
     def a2a(src_of, dst, ssem, rsem, d):
         to = (b + d) % nb
@@ -329,11 +354,11 @@
     au = (lambda t: u_hbm.at[rows(t * part, part)], usub, au_s, au_r)
 
     @pl.loop(1, nb)
-    def _(d):
-        a2a(*au, d).start()
+    def _(i):
+        a2a(*au, farthest_first(i, nb)).start()
 
     u_mine = pltpu.make_async_copy(
-        u_hbm.at[rows(b * part, part)], usub.at[rows(b * part, part)], loc.at[3]
+        u_hbm.at[rows(b * part, part)], usub.at[rows(b * part, part)], loc.at[1]
     )
     u_mine.start()
 
@@ -343,28 +368,33 @@
     lane = jnp.where(lane < n // 2, lane, lane - n).astype(F32)
     shift = []
     for a in (0, 1):
-        row = idx_ref[f + nf * a]
-        shift.append([tab_ref[row, e] for e in range(3)])
+        row = idx_ref[lead + nf * a]
+        shift.append([tab_ref[e, row] for e in range(3)])
     for a in (0, 1):
         fx = freq + shift[a][0]
         fz = lane + shift[a][2]
         hops[rows(a * n, n), :] = fx * fx + fz * fz + SCREEN_SQUARE
     scale = FOUR_PI / n**3
-    per = 2
+    per = 8
 
     @pl.loop(0, n // per)
     def _(k):
-        for a in (0, 1):
-            ys = [k * per + e for e in range(per)]
-            take = [pl.ds(a * n * pitch + y, n, stride=pitch) for y in ys]
-            spectra = along_left([dbuf[t, :] for t in take], lf_ref[...])
+        chains = [(a, k * per + e) for e in range(0, per, 2) for a in (0, 1)]
+        taken, spectra = [], []
+        for a, y in chains:
+            take = [pl.ds(a * n * pitch + y + e, n, stride=pitch) for e in (0, 1)]
+            taken.append(take)
+            spectra.append(along_left([dbuf[t, :] for t in take], lf_ref[...]))
+        screened = []
+        for (a, y), pair in zip(chains, spectra):
             base = hops[pl.ds(a * n, n), :]
-            screened = []
-            for y, spectrum in zip(ys, spectra):
-                fy = jnp.where(y < n // 2, y, y - n).astype(F32) + shift[a][1]
-                screened.append(spectrum * (scale / (base + fy * fy)))
-            fields = along_left(screened, li_ref[...])
-            for t, field in zip(take, fields):
+            both = []
+            for e in (0, 1):
+                fy = jnp.where(y + e < n // 2, y + e, y + e - n).astype(F32) + shift[a][1]
+                both.append(pair[e] * (scale / (base + fy * fy)))
+            screened.append(both)
+        for take, both in zip(taken, screened):
+            for t, field in zip(take, along_left(both, li_ref[...])):
                 dbuf[t, :] = field
 
     def dv(k):
@@ -393,23 +423,25 @@
             return hop(k, piece(toward, 1 - way), way)
         return hop(k, piece(toward, way), way)
 
+    wide = planes
+
     def inverse_planes(s, k):
         total = None
         for a in (0, 1):
-            base = (a * n + s * planes + k * batch) * pitch
+            base = (a * n + s * planes + k * wide) * pitch
             fields = []
-            for q in range(0, batch, 2):
+            for q in range(0, wide, 2):
                 fields += along_left(
                     [dbuf[rows(base + (q + e) * pitch, n), :] for e in (0, 1)], li_ref[...]
                 )
             field = along_last(jnp.concatenate(fields, axis=0), zi_ref[...])
-            p = pfull[rows((a * nf + s) * slab + k * batch * n, batch * n), :]
+            p = pfull[rows((a * nf + s) * slab + k * wide * n, wide * n), :]
             ps = swapped(p)
             real = jnp.where(first_lanes, p, ps)
             imag = jnp.where(first_lanes, -ps, p)
             term = real * field + imag * swapped(field)
             total = term if total is None else total + term
-        vbuf[rows(s * slab + k * batch * n, batch * n), :] = total
+        vbuf[rows(s * slab + k * wide * n, wide * n), :] = total
 
     @pl.loop(0, 2 * nx)
     def _(i):
@@ -417,8 +449,7 @@
         k = i % nx
         s = slab_at(k, jnp.where(own, c, 1 - c))
 
-        @pl.loop(0, planes // batch)
-        def _(q):
+        for q in range(planes // wide):
             inverse_planes(s, q)
 
         @pl.when(jnp.logical_not(own))
@@ -459,8 +490,8 @@
     av = (lambda t: pot_ref.at[rows(t * part, part)], vsub, av_s, av_r)
 
     @pl.loop(1, nb)
-    def _(d):
-        a2a(*av, d).start()
+    def _(i):
+        a2a(*av, farthest_first(i, nb)).start()
 
     vsub[rows(b * part, part), :] = pot_ref[rows(b * part, part), :]
     u_mine.wait()
@@ -487,43 +518,48 @@
         )
     acc = acc[:nb] + acc[nb:]
     acc = (acc[:, : 2 * nb] + acc[:, 2 * nb :]) * (1.0 / n**3)
-    mine[...] = jnp.concatenate([acc, jnp.zeros((nb, width - 2 * nb), F32)], axis=1)
+    folds = width // (2 * nb)
+    tall = nb // folds
+    mine[...] = jnp.concatenate([acc[k * tall : (k + 1) * tall] for k in range(folds)], axis=1)
 
     def mf(d, here=False):
         to = (f + d) % nf
         source = (f - d + nf) % nf
         at = source if here else f
-        return rc(mine, mrow.at[rows(at * nb, nb)], mf_s.at[d], mf_r.at[d], fft=to)
+        return rc(mine, mrow.at[at], mf_s.at[d], mf_r.at[d], fft=to)
 
     def mb(d, here=False):
         to = (b + d) % nb
         source = (b - d + nb) % nb
         at = source if here else b
-        return rc(mcol, mall.at[rows(at * nb, nb)], mb_s.at[d], mb_r.at[d], band=to)
-
-    for d in range(1, nf):
-        mf(d).start()
-    mrow[rows(f * nb, nb), :] = mine[...]
+        return rc(mcol, mall.at[at], mb_s.at[d], mb_r.at[d], band=to)
+
+    for i in range(1, nf):
+        mf(nf // 2 + (i // 2 if i % 2 == 0 else -(i // 2))).start()
+    mrow[f] = mine[...]
     for d in range(1, nf):
         mf(d, True).wait_recv()
-    total = mrow[0:nb, :]
+    total = mrow[0]
     for k in range(1, nf):
-        total += mrow[k * nb : (k + 1) * nb, :]
+        total += mrow[k]
     mcol[...] = total
 
     @pl.loop(1, nb)
-    def _(d):
-        mb(d).start()
-
-    mall[rows(b * nb, nb), :] = mcol[...]
+    def _(i):
+        mb(farthest_first(i, nb)).start()
+
+    mall[b] = mcol[...]
 
     @pl.loop(1, nb)
     def _(d):
         mb(d, True).wait_recv()
 
-    total = mall[0:nb, :]
+    total = mall[0]
     for k in range(1, nb):
-        total += mall[k * nb : (k + 1) * nb, :]
+        total += mall[k]
+    total = jnp.concatenate(
+        [total[:, 2 * nb * k : 2 * nb * (k + 1)] for k in range(folds)], axis=0
+    )
 
     ri = lax.broadcasted_iota(jnp.int32, (nb, nb), 0)
     ci = lax.broadcasted_iota(jnp.int32, (nb, nb), 1)
@@ -567,15 +603,15 @@
     ap = (lambda t: psub.at[rows(t * part, part)], proj_ref, ap_s, ap_r)
 
     @pl.loop(1, nb)
-    def _(d):
-        a2a(*ap, d).start()
+    def _(i):
+        a2a(*ap, farthest_first(i, nb)).start()
 
     proj_ref[rows(b * part, part), :] = psub[rows(b * part, part), :]
 
     @pl.when(jnp.logical_not(alone))
     def _():
-        perm(0).wait_send()
-        perm(1).wait_send()
+        for q in range(quarters):
+            perm(q).wait_send()
 
     for way in (0, 1):
         for h in (0, 1):
@@ -586,12 +622,12 @@
 
     @pl.loop(1, last)
     def _(s):
-        for h in (0, 1):
+        for q in range(quarters):
             for way in (0, 1):
-                agz(s, h, way).wait_send()
-
-    for way in (0, 1):
-        agz(last, way, way).wait_send()
+                agz(s, q, way).wait_send()
+
+    for q in range(quarters):
+        agz(last, q, 2 * q // quarters).wait_send()
 
     @pl.loop(0, nx)
     def _(k):
@@ -620,7 +656,7 @@
     width = orbitals.shape[3]
     slab = orbitals.shape[0] * orbitals.shape[1] * n
     part = slab // nb
-    assert nb == 2 * nf and nf == 8 and orbitals.shape[0] == 1
+    assert nb == 2 * nf and nf == 8 and SPREAD**2 % nf == 1 and orbitals.shape[0] == 1
 
     def call(p, u, *rest):
         any_spec = pl.BlockSpec(memory_space=pl.ANY)
@@ -629,6 +665,7 @@
         dma = pltpu.SemaphoreType.DMA
         out = jax.ShapeDtypeStruct((slab, width), F32)
         half = slab // 2
+        tall = 2 * nb * nb // width
         return pl.pallas_call(
             lambda *refs: kernel(nb, nf, n, *refs),
             out_shape=(out, out),
@@ -644,12 +681,12 @@
                 pltpu.VMEM((slab, width), F32),
                 pltpu.VMEM((slab, width), F32),
                 pltpu.VMEM((slab, width), F32),
-                pltpu.VMEM((nb, width), F32),
-                pltpu.VMEM((nf * nb, width), F32),
-                pltpu.VMEM((nb, width), F32),
-                pltpu.VMEM((nb * nb, width), F32),
-                dma((2,)), dma((2,)), dma((4,)),
-                dma((nb // 2 + 1, 2, 2)), dma((nb // 2 + 1, 2, 2)),
+                pltpu.VMEM((tall, width), F32),
+                pltpu.VMEM((nf, tall, width), F32),
+                pltpu.VMEM((tall, width), F32),
+                pltpu.VMEM((nb, tall, width), F32),
+                dma((4,)), dma((4,)), dma((6,)),
+                dma((nb // 2 + 1, 4, 2)), dma((nb // 2 + 1, 4, 2)),
                 dma((2, 2, 2)), dma((2, 2, 2)),
                 dma((4,)), dma((4,)), dma((4,)), dma((4,)), dma((6,)), dma((6,)),
                 dma((nb,)), dma((nb,)), dma((nb,)), dma((nb,)), dma((nb,)), dma((nb,)),
@@ -665,7 +702,7 @@
     ]
     pot, proj = call(
         partners.reshape(slab, width), orbitals.reshape(slab, width), *tables,
-        shift_table, shift_index,
+        shift_table.T, shift_index,
     )
     return pot.reshape(orbitals.shape), proj.reshape(orbitals.shape)
 

time: 183 us -> 153 us (0.84)
  Pallas kernels: 178 us -> 149 us
    pallas_call x1, Pallas kernels: 178 us -> 149 us  [call(): pl.pallas_call(lambda *refs: kernel(nb, nf, n, *refs), out_shape=(out, ou...]
    unnamed x7 -> x4, local copies, waits for them, and re-layouts: 3.77 us -> 2.42 us
where the time goes in v2:
time: 153 us; the launch traced here: 152 us
  Pallas kernels  149 us (97%)
  local copies, waits for them, and re-layouts  2.42 us (2%)
    pallas_call x1, Pallas kernels, call(): pl.pallas_call(lambda *refs: kernel(nb, nf, n, *refs), out_shape=(out, ou...  149 us

profile of v2, /device:TPU:33, one launch (start us, length us, event | category | flops | bytes accessed | tf_op | source)
XLA Modules:
  0.0 151.9 jit_solution(11443267857304432225)
XLA Ops:
  0.6 148.8 %exchange.1 = (f32[512,128]{1,0:T(8,128)}, f32[512,128]{1,0:T(8,128)}) custom-call(f32[512,128]{1,0:T(8,128)} %bitcast.5, f32[512,128]{1,0:T(8,128)} %bitcast.6, bf16[256,256]{1,0:T(8,128)(2,1)} %constant.8.clone.refs_2_, bf16[256,256]{1,0:T(8,128)(2,1)} %constant.9.clone.refs_3_, bf16[128,256]{1,0:T(8,128)(2,1)} %constant.10.clone.refs_4_, ...), custom_call_target="tpu_custom_call" | custom-call | tf_op jit(solution)/shard_map/exchange/pallas_call | solution.py:669
  149.4 0.0 copy-start
  149.4 1.7 %copy.12 = f32[1,8,64,128]{3,2,1,0:T(8,128)} copy(f32[1,8,64,128]{3,2,1,0:T(8,128)} %bitcast.8) | data formatting | bytes 524288
  151.1 0.0 copy-done
  151.1 0.7 copy.13
Async XLA Ops:
  149.4 1.7 %copy-start = (f32[512,128]{1,0:T(8,128)S(1)}, f32[512,128]{1,0:T(8,128)}, u32[]{:S(2)}) copy-start(f32[512,128]{1,0:T(8,128)} %get-tuple-element.5) | copy-start | bytes 786436

commit v3 on v2

--- a/solution.py
+++ b/solution.py
@@ -96,8 +96,7 @@
     nb, nf, n, p_hbm, u_hbm, zf_ref, zi_ref, lf_ref, li_ref, tab_ref, idx_ref,
     pot_ref, proj_ref,
     pfull, ufull, dbuf, vbuf, d2d, hops, usub, vsub, psub, mine, mrow, mcol, mall,
-    perm_s, perm_r, loc, agz_s, agz_r, agx_s, agx_r, du_s, du_r, dv_s, dv_r, rs_s, rs_r,
-    au_s, au_r, av_s, av_r, ap_s, ap_r, mf_s, mf_r, mb_s, mb_r,
+    perm_r, loc, agz_r, agx_r, du_r, dv_r, rs_r, many,
 ):
     slab = p_hbm.shape[0]
     half = slab // 2
@@ -135,6 +134,16 @@
             device_id_type=MESH,
         )
 
+    perm_s, agz_s, agx_s, du_s, dv_s, rs_s = [many.at[k] for k in range(6)]
+    au_s, av_s, ap_s, mf_s, mb_s = [many.at[k] for k in range(6, 11)]
+    au_r, av_r, ap_r, mf_r, mb_r = [many.at[k] for k in range(11, 16)]
+
+    def all_sent(ref, sem):
+        rc(ref, ref, sem, sem, fft=mate).wait_send()
+
+    def all_here(ref, sem):
+        rc(ref, ref, sem, sem, fft=mate).wait_recv()
+
     barrier = pltpu.get_barrier_semaphore()
 
     def greet(**dev):
@@ -162,14 +171,14 @@
         return rc(
             p_hbm.at[rows(q * quarter, quarter)],
             pfull.at[rows(to_slot * slab + q * quarter, quarter)],
-            perm_s.at[q], perm_r.at[q], band=to_band, fft=to_fft,
+            perm_s, perm_r.at[q], band=to_band, fft=to_fft,
         )
 
     def perm_here(q):
         return rc(
             p_hbm.at[rows(q * quarter, quarter)],
             pfull.at[rows(place(slot) * slab + q * quarter, quarter)],
-            perm_s.at[q], perm_r.at[q], band=from_band, fft=from_fft,
+            perm_s, perm_r.at[q], band=from_band, fft=from_fft,
         )
 
     def perm_local(q):
@@ -194,35 +203,35 @@
     def agx1(h, way):
         return rc(
             u_hbm.at[rows(h * half, half)], ufull.at[rows(f * slab + h * half, half)],
-            agx_s.at[0, h, way], agx_r.at[0, h, way], fft=fright if way == 0 else fleft,
+            agx_s, agx_r.at[0, h, way], fft=fright if way == 0 else fleft,
         )
 
     def agx1_here(h, way):
         owner = slab_of(nx - 1 if way == 0 else 1, c)
         return rc(
             u_hbm.at[rows(h * half, half)], ufull.at[rows(owner * slab + h * half, half)],
-            agx_s.at[0, h, way], agx_r.at[0, h, way], fft=fright if way == 0 else fleft,
+            agx_s, agx_r.at[0, h, way], fft=fright if way == 0 else fleft,
         )
 
     def agx2(way):
         owner = slab_of(nx - 1 if way == 0 else 1, c)
         piece = ufull.at[rows(owner * slab + way * half, half)]
         return rc(
-            piece, piece, agx_s.at[1, 0, way], agx_r.at[1, 0, way],
+            piece, piece, agx_s, agx_r.at[1, 0, way],
             fft=fright if way == 0 else fleft,
         )
 
     def agx2_here(way):
         piece = ufull.at[rows(slab_of(2, c) * slab + way * half, half)]
         return rc(
-            piece, piece, agx_s.at[1, 0, way], agx_r.at[1, 0, way],
+            piece, piece, agx_s, agx_r.at[1, 0, way],
             fft=fright if way == 0 else fleft,
         )
 
     def du(k, core):
         piece = ufull.at[rows(slab_of((0, nx - 1, 1, 2)[k], core) * slab, slab)]
         src = u_hbm if (k == 0) else piece
-        return rc(src, piece, du_s.at[k], du_r.at[k], fft=mate)
+        return rc(src, piece, du_s, du_r.at[k], fft=mate)
 
     du(0, c).start()
 
@@ -230,7 +239,7 @@
         owner = (slot - (s - 1) + nb) % nb if way == 0 else (slot + (s - 1)) % nb
         piece = pfull.at[rows(place(owner) * slab + q * quarter, quarter)]
         return rc(
-            piece, piece, agz_s.at[s, q, way], agz_r.at[s, q, way],
+            piece, piece, agz_s, agz_r.at[s, q, way],
             band=right if way == 0 else left,
         )
 
@@ -238,7 +247,7 @@
         owner = (slot - s + nb) % nb if way == 0 else (slot + s) % nb
         piece = pfull.at[rows(place(owner) * slab + q * quarter, quarter)]
         return rc(
-            piece, piece, agz_s.at[s, q, way], agz_r.at[s, q, way],
+            piece, piece, agz_s, agz_r.at[s, q, way],
             band=right if way == 0 else left,
         )
 
@@ -274,6 +283,8 @@
     for way in (0, 1):
         agx1_here(1 - way, way).wait_recv()
         du(1 + way, c).start()
+    for q in range(quarters):
+        forward(4, q)
     for way in (0, 1):
         agx2_here(way).wait_recv()
     du(3, c).start()
@@ -309,7 +320,7 @@
         ready = per_slab * (2 * (t // quarters + first - 2) + 1)
         return jnp.minimum(jnp.minimum(2 * (t + 1), ready), nb * per_slab)
 
-    first = 4
+    first = 5
 
     @pl.loop(0, quarters * (last + 2 - first) + 1)
     def _(t):
@@ -342,25 +353,37 @@
             owner = jnp.where(order % 2 == 1, slot + far, slot - far + nb) % nb
             forward_planes(place(owner), k)
 
-    def a2a(src_of, dst, ssem, rsem, d):
+    bit = part // 2
+
+    def in_slab(t, h):
+        return rows(h * half + t * bit, bit)
+
+    def in_parts(t, h):
+        return rows(t * part + h * bit, bit)
+
+    def spread(src, dst, ssem, rsem, h, d):
         to = (b + d) % nb
-        return rc(src_of(to), dst.at[rows(b * part, part)], ssem.at[d], rsem.at[d], band=to)
-
-    def a2a_here(src_of, dst, ssem, rsem, d):
+        return rc(src.at[in_slab(to, h)], dst.at[in_parts(b, h)], ssem, rsem, band=to)
+
+    def gather(h, d):
         to = (b + d) % nb
-        source = (b - d + nb) % nb
-        return rc(src_of(to), dst.at[rows(source * part, part)], ssem.at[d], rsem.at[d], band=to)
-
-    au = (lambda t: u_hbm.at[rows(t * part, part)], usub, au_s, au_r)
+        return rc(psub.at[in_parts(to, h)], proj_ref.at[in_slab(b, h)], ap_s, ap_r, band=to)
+
+    au = (u_hbm, usub, au_s, au_r)
+    av = (pot_ref, vsub, av_s, av_r)
 
     @pl.loop(1, nb)
     def _(i):
-        a2a(*au, farthest_first(i, nb)).start()
-
-    u_mine = pltpu.make_async_copy(
-        u_hbm.at[rows(b * part, part)], usub.at[rows(b * part, part)], loc.at[1]
-    )
-    u_mine.start()
+        for h in (0, 1):
+            spread(*au, h, farthest_first(i, nb)).start()
+
+    def u_mine(h):
+        return pltpu.make_async_copy(
+            u_hbm.at[in_slab(b, h)], usub.at[in_parts(b, h)], loc.at[1 if h == 0 else 6]
+        )
+
+    for h in (0, 1):
+        u_mine(h).start()
 
     freq = lax.broadcasted_iota(jnp.int32, (n, width), 0)
     freq = jnp.where(freq < n // 2, freq, freq - n).astype(F32)
@@ -397,112 +420,111 @@
             for t, field in zip(take, along_left(both, li_ref[...])):
                 dbuf[t, :] = field
 
-    def dv(k):
-        src = vbuf.at[rows(slab_at(k, 1 - c) * slab, slab)]
-        return rc(src, d2d.at[rows(k * slab, slab)], dv_s.at[k], dv_r.at[k], fft=mate)
-
-    def slab_at(k, core):
-        dx = jnp.where(k == 0, 2, jnp.where(k == 1, 1, jnp.where(k == 2, nx - 1, 0)))
-        return slab_of(dx, core)
-
-    def hop(k, src, way):
-        return rc(
-            src, hops.at[rows(2 * n + k * half, half)], rs_s.at[k], rs_r.at[k],
-            fft=fright if way == 0 else fleft,
-        )
-
-    def piece(dx, h):
-        return vbuf.at[rows(slab_of(dx, c) * slab + h * half, half)]
-
-    def hop_of(k):
+    order = (2, 1, nx - 1, 0)
+
+    def dv(h, k):
+        src = vbuf.at[rows(slab_of(order[k], 1 - c) * slab + h * half, half)]
+        return rc(
+            src, d2d.at[rows(k * slab + h * half, half)], dv_s, dv_r.at[h, k], fft=mate
+        )
+
+    def landing(h, k):
+        return rows(2 * n + (h * 6 + k) * quarter, quarter)
+
+    def own_rows(dx, h, e):
+        return rows(slab_of(dx, c) * slab + h * half + e * quarter, quarter)
+
+    def hop(h, k):
         way = k % 2
         toward = 1 if way == 0 else nx - 1
-        if k < 2:
-            return hop(k, piece(2, way), way)
-        if k < 4:
-            return hop(k, piece(toward, 1 - way), way)
-        return hop(k, piece(toward, way), way)
-
-    wide = planes
-
-    def inverse_planes(s, k):
+        piece = own_rows(2 if k < 2 else toward, h, 1 - way if k in (2, 3) else way)
+        return rc(
+            vbuf.at[piece], hops.at[landing(h, k)], rs_s, rs_r.at[h, k],
+            fft=fright if way == 0 else fleft,
+        )
+
+    def inverse_halves(h, pair, core):
+        at = [slab_of(order[k], core) for k in pair]
         total = None
         for a in (0, 1):
-            base = (a * n + s * planes + k * wide) * pitch
             fields = []
-            for q in range(0, wide, 2):
-                fields += along_left(
-                    [dbuf[rows(base + (q + e) * pitch, n), :] for e in (0, 1)], li_ref[...]
-                )
+            for s in at:
+                base = (a * n + s * planes + h * (planes // 2)) * pitch
+                for e in range(0, planes // 2, 2):
+                    fields += along_left(
+                        [dbuf[rows(base + (e + g) * pitch, n), :] for g in (0, 1)], li_ref[...]
+                    )
             field = along_last(jnp.concatenate(fields, axis=0), zi_ref[...])
-            p = pfull[rows((a * nf + s) * slab + k * wide * n, wide * n), :]
+            p = jnp.concatenate(
+                [pfull[rows((a * nf + s) * slab + h * half, half), :] for s in at], axis=0
+            )
             ps = swapped(p)
             real = jnp.where(first_lanes, p, ps)
             imag = jnp.where(first_lanes, -ps, p)
             term = real * field + imag * swapped(field)
             total = term if total is None else total + term
-        vbuf[rows(s * slab + k * wide * n, wide * n), :] = total
-
-    @pl.loop(0, 2 * nx)
-    def _(i):
-        own = i >= nx
-        k = i % nx
-        s = slab_at(k, jnp.where(own, c, 1 - c))
-
-        for q in range(planes // wide):
-            inverse_planes(s, q)
-
-        @pl.when(jnp.logical_not(own))
+        for k, s in enumerate(at):
+            vbuf[rows(s * slab + h * half, half), :] = total[k * half : (k + 1) * half]
+
+    def relay(h):
+        for way in (0, 1):
+            hop(h, way).wait_recv()
+            toward = own_rows(1 if way == 0 else nx - 1, h, way)
+            vbuf[toward, :] += hops[landing(h, way), :]
+            hop(h, 4 + way).start()
+
+    def with_mate(h, k):
+        dv(h, k).wait_recv()
+        own = rows(slab_of(order[k], c) * slab + h * half, half)
+        vbuf[own, :] += d2d[rows(k * slab + h * half, half), :]
+
+    @pl.loop(0, 2)
+    def _(h):
+        inverse_halves(h, (0, 1), 1 - c)
+        dv(h, 0).start()
+        dv(h, 1).start()
+        inverse_halves(h, (0, 1), c)
+        inverse_halves(h, (2, 3), 1 - c)
+        dv(h, 2).start()
+        dv(h, 3).start()
+
+        @pl.when(h == 1)
         def _():
-            dv(k).start()
-
-        @pl.when(own)
-        def _():
-            dv(k).wait_recv()
-            vbuf[rows(s * slab, slab), :] += d2d[rows(k * slab, slab), :]
-
-        @pl.when(i == nx)
-        def _():
-            hop_of(0).start()
-            hop_of(1).start()
-
-        @pl.when(i == nx + 1)
-        def _():
-            hop_of(2).start()
-
-        @pl.when(i == nx + 2)
-        def _():
-            hop_of(3).start()
-
-    def arrived(k):
-        return hops[rows(2 * n + k * half, half), :]
-
-    for way in (0, 1):
-        hop_of(way).wait_recv()
-        toward = slab_of(1 if way == 0 else nx - 1, c)
-        vbuf[rows(toward * slab + way * half, half), :] += arrived(way)
-        hop_of(4 + way).start()
-    for k in (2, 3, 4, 5):
-        hop_of(k).wait_recv()
-    pot_ref[0:half, :] = vbuf[rows(f * slab, half), :] + arrived(3) + arrived(4)
-    pot_ref[half:slab, :] = vbuf[rows(f * slab + half, half), :] + arrived(2) + arrived(5)
-
-    av = (lambda t: pot_ref.at[rows(t * part, part)], vsub, av_s, av_r)
-
-    @pl.loop(1, nb)
-    def _(i):
-        a2a(*av, farthest_first(i, nb)).start()
-
-    vsub[rows(b * part, part), :] = pot_ref[rows(b * part, part), :]
-    u_mine.wait()
-
-    @pl.loop(1, nb)
-    def _(d):
-        a2a_here(*au, d).wait_recv()
-
-    @pl.loop(1, nb)
-    def _(d):
-        a2a_here(*av, d).wait_recv()
+            relay(0)
+
+        with_mate(h, 0)
+        hop(h, 0).start()
+        hop(h, 1).start()
+        with_mate(h, 1)
+        hop(h, 2).start()
+        inverse_halves(h, (2, 3), c)
+        with_mate(h, 2)
+        hop(h, 3).start()
+        with_mate(h, 3)
+
+    for h in (0, 1):
+        if h == 1:
+            relay(1)
+        for k in (2, 3, 4, 5):
+            hop(h, k).wait_recv()
+        pot_ref[rows(h * half, quarter), :] = (
+            vbuf[own_rows(0, h, 0), :] + hops[landing(h, 3), :] + hops[landing(h, 4), :]
+        )
+        pot_ref[rows(h * half + quarter, quarter), :] = (
+            vbuf[own_rows(0, h, 1), :] + hops[landing(h, 2), :] + hops[landing(h, 5), :]
+        )
+
+        @pl.loop(1, nb)
+        def _(m):
+            spread(*av, h, farthest_first(m, nb)).start()
+
+    for h in (0, 1):
+        vsub[in_parts(b, h), :] = pot_ref[in_slab(b, h), :]
+        u_mine(h).wait()
+
+    others = pl.ds(0, (nb - 1) * part)
+    all_here(usub.at[others], au_r)
+    all_here(vsub.at[others], av_r)
 
     group = 4
     acc = jnp.zeros((2 * nb, 4 * nb), F32)
@@ -522,23 +544,18 @@
     tall = nb // folds
     mine[...] = jnp.concatenate([acc[k * tall : (k + 1) * tall] for k in range(folds)], axis=1)
 
-    def mf(d, here=False):
+    def mf(d):
         to = (f + d) % nf
-        source = (f - d + nf) % nf
-        at = source if here else f
-        return rc(mine, mrow.at[at], mf_s.at[d], mf_r.at[d], fft=to)
-
-    def mb(d, here=False):
+        return rc(mine, mrow.at[f], mf_s, mf_r, fft=to)
+
+    def mb(d):
         to = (b + d) % nb
-        source = (b - d + nb) % nb
-        at = source if here else b
-        return rc(mcol, mall.at[at], mb_s.at[d], mb_r.at[d], band=to)
+        return rc(mcol, mall.at[b], mb_s, mb_r, band=to)
 
     for i in range(1, nf):
         mf(nf // 2 + (i // 2 if i % 2 == 0 else -(i // 2))).start()
     mrow[f] = mine[...]
-    for d in range(1, nf):
-        mf(d, True).wait_recv()
+    all_here(mrow.at[pl.ds(0, nf - 1)], mf_r)
     total = mrow[0]
     for k in range(1, nf):
         total += mrow[k]
@@ -550,9 +567,7 @@
 
     mall[b] = mcol[...]
 
-    @pl.loop(1, nb)
-    def _(d):
-        mb(d, True).wait_recv()
+    all_here(mall.at[pl.ds(0, nb - 1)], mb_r)
 
     total = mall[0]
     for k in range(1, nb):
@@ -600,54 +615,29 @@
         for e in range(group):
             psub[pl.ds(g + e, nb, stride=part), :] = out[:, e * width : (e + 1) * width]
 
-    ap = (lambda t: psub.at[rows(t * part, part)], proj_ref, ap_s, ap_r)
-
     @pl.loop(1, nb)
     def _(i):
-        a2a(*ap, farthest_first(i, nb)).start()
-
-    proj_ref[rows(b * part, part), :] = psub[rows(b * part, part), :]
+        for h in (0, 1):
+            gather(h, farthest_first(i, nb)).start()
+
+    for h in (0, 1):
+        proj_ref[in_slab(b, h), :] = psub[in_parts(b, h), :]
 
     @pl.when(jnp.logical_not(alone))
     def _():
-        for q in range(quarters):
-            perm(q).wait_send()
-
-    for way in (0, 1):
-        for h in (0, 1):
-            agx1(h, way).wait_send()
-        agx2(way).wait_send()
-    for k in range(4):
-        du(k, c).wait_send()
-
-    @pl.loop(1, last)
-    def _(s):
-        for q in range(quarters):
-            for way in (0, 1):
-                agz(s, q, way).wait_send()
-
-    for q in range(quarters):
-        agz(last, q, 2 * q // quarters).wait_send()
-
-    @pl.loop(0, nx)
-    def _(k):
-        dv(k).wait_send()
-
-    for k in range(6):
-        hop_of(k).wait_send()
-    for d in range(1, nf):
-        mf(d).wait_send()
-
-    @pl.loop(1, nb)
-    def _(d):
-        a2a(*au, d).wait_send()
-        a2a(*av, d).wait_send()
-        mb(d).wait_send()
-        a2a(*ap, d).wait_send()
-
-    @pl.loop(1, nb)
-    def _(d):
-        a2a_here(*ap, d).wait_recv()
+        all_sent(pfull.at[pl.ds(0, slab)], perm_s)
+
+    all_sent(pfull.at[pl.ds(0, (nb - 1) * slab)], agz_s)
+    all_sent(ufull.at[pl.ds(0, (nx - 1) * slab)], agx_s)
+    all_sent(ufull.at[pl.ds(0, nx * slab)], du_s)
+    all_sent(vbuf.at[pl.ds(0, nx * slab)], dv_s)
+    all_sent(vbuf.at[pl.ds(0, (nx - 1) * slab)], rs_s)
+    all_sent(usub.at[others], au_s)
+    all_sent(vsub.at[others], av_s)
+    all_sent(mrow.at[pl.ds(0, nf - 1)], mf_s)
+    all_sent(mall.at[pl.ds(0, nb - 1)], mb_s)
+    all_sent(psub.at[others], ap_s)
+    all_here(proj_ref.at[others], ap_r)
 
 
 def body(mesh, orbitals, partners, shift_table, shift_index):
@@ -663,7 +653,7 @@
         vmem = pl.BlockSpec(memory_space=pltpu.VMEM)
         smem = pl.BlockSpec(memory_space=pltpu.SMEM)
         dma = pltpu.SemaphoreType.DMA
-        out = jax.ShapeDtypeStruct((slab, width), F32)
+        out = pltpu.VMEM((slab, width), F32)
         half = slab // 2
         tall = 2 * nb * nb // width
         return pl.pallas_call(
@@ -685,12 +675,8 @@
                 pltpu.VMEM((nf, tall, width), F32),
                 pltpu.VMEM((tall, width), F32),
                 pltpu.VMEM((nb, tall, width), F32),
-                dma((4,)), dma((4,)), dma((6,)),
-                dma((nb // 2 + 1, 4, 2)), dma((nb // 2 + 1, 4, 2)),
-                dma((2, 2, 2)), dma((2, 2, 2)),
-                dma((4,)), dma((4,)), dma((4,)), dma((4,)), dma((6,)), dma((6,)),
-                dma((nb,)), dma((nb,)), dma((nb,)), dma((nb,)), dma((nb,)), dma((nb,)),
-                dma((nf,)), dma((nf,)), dma((nb,)), dma((nb,)),
+                dma((4,)), dma((7,)), dma((nb // 2 + 1, 4, 2)), dma((2, 2, 2)), dma((4,)),
+                dma((2, 4)), dma((2, 6)), dma((16,)),
             ],
             compiler_params=pltpu.CompilerParams(collective_id=0, has_side_effects=True),
             name="exchange",

time: 153 us -> 146 us (0.954)
  Pallas kernels: 149 us -> 143 us
    pallas_call x1, Pallas kernels: 149 us -> 143 us  [call(): pl.pallas_call(lambda *refs: kernel(nb, nf, n, *refs), out_shape=(out, ou...]
where the time goes in v3:
time: 146 us
  Pallas kernels  143 us (98%)
    pallas_call x1, Pallas kernels, call(): pl.pallas_call(lambda *refs: kernel(nb, nf, n, *refs), out_shape=(out, ou...  143 us

profile of v3, /device:TPU:33, one launch (start us, length us, event | category | flops | bytes accessed | tf_op | source)
XLA Modules:
  0.0 145.5 jit_solution(8747692467538342760)
XLA Ops:
  0.6 143.5 %exchange.1 = (f32[512,128]{1,0:T(8,128)S(1)}, f32[512,128]{1,0:T(8,128)S(1)}) custom-call(f32[512,128]{1,0:T(8,128)} %bitcast.7, f32[512,128]{1,0:T(8,128)} %bitcast.8, bf16[256,256]{1,0:T(8,128)(2,1)} %constant.8.clone.refs_2_, bf16[256,256]{1,0:T(8,128)(2,1)} %constant.9.clone.refs_3_, bf16[128,256]{1,0:T(8,128)(2,1)} %constant.10.clone.refs_4_, ...), custom_call_target="tpu_custom_call" | custom-call | tf_op jit(solution)/shard_map/exchange/pallas_call | solution.py:659
  144.1 0.7 copy.12
  144.8 0.7 copy.13

commit v4 on v3

--- a/solution.py
+++ b/solution.py
@@ -93,9 +93,9 @@
 
 
 def kernel(
-    nb, nf, n, p_hbm, u_hbm, zf_ref, zi_ref, lf_ref, li_ref, tab_ref, idx_ref,
+    nb, nf, n, p_hbm, u_hbm, zf_hbm, zi_hbm, lf_hbm, li_hbm, tab_ref, idx_ref,
     pot_ref, proj_ref,
-    pfull, ufull, dbuf, vbuf, d2d, hops, usub, vsub, psub, mine, mrow, mcol, mall,
+    zf_ref, zi_ref, lf_ref, li_ref, pfull, ufull, dbuf, vbuf, d2d, hops, usub, vsub, psub, mine, mrow, mcol, mall,
     perm_r, loc, agz_r, agx_r, du_r, dv_r, rs_r, many,
 ):
     slab = p_hbm.shape[0]
@@ -160,6 +160,14 @@
         greet(band=to_band, fft=to_fft)
         greet(band=from_band, fft=from_fft)
 
+    tables = [
+        pltpu.make_async_copy(src, dst, loc.at[7 + k])
+        for k, (src, dst) in enumerate(
+            ((zf_hbm, zf_ref), (zi_hbm, zi_ref), (lf_hbm, lf_ref), (li_hbm, li_ref))
+        )
+    ]
+    for table in tables:
+        table.start()
     u_local = pltpu.make_async_copy(u_hbm, ufull.at[rows(f * slab, slab)], loc.at[0])
     u_local.start()
     pl.semaphore_wait(barrier, jnp.where(alone, 5, 7))
@@ -289,6 +297,8 @@
         agx2_here(way).wait_recv()
     du(3, c).start()
     u_local.wait()
+    for table in tables:
+        table.wait()
     for k in range(4):
         du(k, 1 - c).wait_recv()
 
@@ -322,37 +332,33 @@
 
     first = 5
 
-    @pl.loop(0, quarters * (last + 2 - first) + 1)
-    def _(t):
-        s, q = first + t // quarters, t % quarters
-
-        @pl.when(s < last)
-        def _():
-            forward(s, q)
-
-        @pl.when(s == last)
-        def _():
-            for way in (0, 1):
-                agz_here(s - 1, q, way).wait_recv()
-
-                @pl.when(2 * q // quarters == way)
-                def _():
-                    agz(s, q, way).start()
-
-        @pl.when(s == last + 1)
-        def _():
-            for way in (0, 1):
-                @pl.when(2 * q // quarters == way)
-                def _():
-                    agz_here(last, q, way).wait_recv()
-
-        @pl.loop(jnp.where(t == 0, 0, items_ready(t - 1)), items_ready(t))
+    def items(start, stop):
+        @pl.loop(start, stop)
         def _(w):
             order, k = w // per_slab, w % per_slab
             far = (order + 1) // 2
             owner = jnp.where(order % 2 == 1, slot + far, slot - far + nb) % nb
             forward_planes(place(owner), k)
 
+    @pl.loop(0, quarters * (last + 1 - first))
+    def _(t):
+        s, q = first + t // quarters, t % quarters
+
+        @pl.when(s < last)
+        def _():
+            forward(s, q)
+
+        @pl.when(s == last)
+        def _():
+            for way in (0, 1):
+                agz_here(s - 1, q, way).wait_recv()
+
+                @pl.when(2 * q // quarters == way)
+                def _():
+                    agz(s, q, way).start()
+
+        items(jnp.where(t == 0, 0, items_ready(t - 1)), items_ready(t))
+
     bit = part // 2
 
     def in_slab(t, h):
@@ -372,53 +378,61 @@
     au = (u_hbm, usub, au_s, au_r)
     av = (pot_ref, vsub, av_s, av_r)
 
-    @pl.loop(1, nb)
-    def _(i):
-        for h in (0, 1):
-            spread(*au, h, farthest_first(i, nb)).start()
-
     def u_mine(h):
         return pltpu.make_async_copy(
             u_hbm.at[in_slab(b, h)], usub.at[in_parts(b, h)], loc.at[1 if h == 0 else 6]
         )
-
-    for h in (0, 1):
-        u_mine(h).start()
 
     freq = lax.broadcasted_iota(jnp.int32, (n, width), 0)
     freq = jnp.where(freq < n // 2, freq, freq - n).astype(F32)
     lane = lax.broadcasted_iota(jnp.int32, (n, width), 1) % n
     lane = jnp.where(lane < n // 2, lane, lane - n).astype(F32)
-    shift = []
-    for a in (0, 1):
+    scale = FOUR_PI / n**3
+    per = 16
+    done = items_ready(quarters * (last + 1 - first) - 1)
+    before = (nb - 1) * per_slab
+
+    @pl.loop(0, 2)
+    def _(m):
+        @pl.when(m == 1)
+        def _():
+            for q in range(quarters):
+                agz_here(last, q, 2 * q // quarters).wait_recv()
+
+            @pl.loop(1, nb)
+            def _(i):
+                for h in (0, 1):
+                    spread(*au, h, farthest_first(i, nb)).start()
+
+            for h in (0, 1):
+                u_mine(h).start()
+
+        items(jnp.where(m == 0, done, before), jnp.where(m == 0, before, nb * per_slab))
+        a = (slot // nf + m) % 2
         row = idx_ref[lead + nf * a]
-        shift.append([tab_ref[e, row] for e in range(3)])
-    for a in (0, 1):
-        fx = freq + shift[a][0]
-        fz = lane + shift[a][2]
-        hops[rows(a * n, n), :] = fx * fx + fz * fz + SCREEN_SQUARE
-    scale = FOUR_PI / n**3
-    per = 8
-
-    @pl.loop(0, n // per)
-    def _(k):
-        chains = [(a, k * per + e) for e in range(0, per, 2) for a in (0, 1)]
-        taken, spectra = [], []
-        for a, y in chains:
-            take = [pl.ds(a * n * pitch + y + e, n, stride=pitch) for e in (0, 1)]
-            taken.append(take)
-            spectra.append(along_left([dbuf[t, :] for t in take], lf_ref[...]))
-        screened = []
-        for (a, y), pair in zip(chains, spectra):
-            base = hops[pl.ds(a * n, n), :]
-            both = []
-            for e in (0, 1):
-                fy = jnp.where(y + e < n // 2, y + e, y + e - n).astype(F32) + shift[a][1]
-                both.append(pair[e] * (scale / (base + fy * fy)))
-            screened.append(both)
-        for take, both in zip(taken, screened):
-            for t, field in zip(take, along_left(both, li_ref[...])):
-                dbuf[t, :] = field
+        qx, qy, qz = [tab_ref[e, row] for e in range(3)]
+        fx, fz = freq + qx, lane + qz
+        hops[pl.ds(0, n), :] = fx * fx + fz * fz + SCREEN_SQUARE
+
+        @pl.loop(0, n // per)
+        def _(k):
+            taken, spectra = [], []
+            for y in range(0, per, 2):
+                take = [pl.ds(a * n * pitch + k * per + y + e, n, stride=pitch) for e in (0, 1)]
+                taken.append(take)
+                spectra.append(along_left([dbuf[t, :] for t in take], lf_ref[...]))
+            base = hops[pl.ds(0, n), :]
+            screened = []
+            for y, pair in zip(range(0, per, 2), spectra):
+                both = []
+                for e in (0, 1):
+                    at = k * per + y + e
+                    fy = jnp.where(at < n // 2, at, at - n).astype(F32) + qy
+                    both.append(pair[e] * (scale / (base + fy * fy)))
+                screened.append(both)
+            for take, both in zip(taken, screened):
+                for t, field in zip(take, along_left(both, li_ref[...])):
+                    dbuf[t, :] = field
 
     order = (2, 1, nx - 1, 0)
 
@@ -592,12 +606,14 @@
     zero = jnp.zeros((nb, nb), F32)
     work = jnp.concatenate([hre, him, eye, zero], axis=1)
     other = jnp.concatenate([-him, hre, zero, eye], axis=1)
-    row_at = lax.broadcasted_iota(jnp.int32, (nb, 1), 0)
+    below = lax.broadcasted_iota(jnp.int32, work.shape, 0)
     for k in range(nb):
-        pivot = work[k : k + 1, k : k + 1]
-        cre = jnp.where(row_at > k, work[:, k : k + 1], 0.0) / pivot
-        cim = jnp.where(row_at > k, work[:, nb + k : nb + k + 1], 0.0) / pivot
-        row, rot = work[k : k + 1, :], other[k : k + 1, :]
+        inverse = 1.0 / jnp.broadcast_to(work[k : k + 1, k : k + 1], (1, 4 * nb))
+        row, rot = work[k : k + 1, :] * inverse, other[k : k + 1, :] * inverse
+        cre = jnp.where(below > k, jnp.broadcast_to(work[:, k : k + 1], work.shape), 0.0)
+        cim = jnp.where(
+            below > k, jnp.broadcast_to(work[:, nb + k : nb + k + 1], work.shape), 0.0
+        )
         work = work - (cre * row + cim * rot)
         other = other - (cre * rot - cim * row)
     pivots = jnp.sum(work[:, :nb] * eye, axis=1, keepdims=True)
@@ -659,9 +675,9 @@
         return pl.pallas_call(
             lambda *refs: kernel(nb, nf, n, *refs),
             out_shape=(out, out),
-            in_specs=[any_spec, any_spec, vmem, vmem, vmem, vmem, smem, smem],
+            in_specs=[any_spec] * 6 + [smem, smem],
             out_specs=(vmem, vmem),
-            scratch_shapes=[
+            scratch_shapes=[pltpu.VMEM(t.shape, BF) for t in rest[:4]] + [
                 pltpu.VMEM((nb * slab, width), F32),
                 pltpu.VMEM((nf * slab, width), F32),
                 pltpu.VMEM((2 * n * (n + PAD), width), F32),
@@ -675,7 +691,7 @@
                 pltpu.VMEM((nf, tall, width), F32),
                 pltpu.VMEM((tall, width), F32),
                 pltpu.VMEM((nb, tall, width), F32),
-                dma((4,)), dma((7,)), dma((nb // 2 + 1, 4, 2)), dma((2, 2, 2)), dma((4,)),
+                dma((4,)), dma((11,)), dma((nb // 2 + 1, 4, 2)), dma((2, 2, 2)), dma((4,)),
                 dma((2, 4)), dma((2, 6)), dma((16,)),
             ],
             compiler_params=pltpu.CompilerParams(collective_id=0, has_side_effects=True),

time: 146 us -> 141 us (0.966)
  Pallas kernels: 143 us -> 139 us
    pallas_call x1, Pallas kernels: 143 us -> 139 us  [call(): pl.pallas_call(lambda *refs: kernel(nb, nf, n, *refs), out_shape=(out, ou...]
where the time goes in v4:
time: 141 us
  Pallas kernels  139 us (99%)
  local copies, waits for them, and re-layouts  1.41 us (1%)
    pallas_call x1, Pallas kernels, call(): pl.pallas_call(lambda *refs: kernel(nb, nf, n, *refs), out_shape=(out, ou...  139 us

profile of v4, /device:TPU:33, one launch (start us, length us, event | category | flops | bytes accessed | tf_op | source)
XLA Modules:
  0.0 141.0 jit_solution(9878185859977232977)
XLA Ops:
  0.6 138.9 %exchange.1 = (f32[512,128]{1,0:T(8,128)S(1)}, f32[512,128]{1,0:T(8,128)S(1)}) custom-call(f32[512,128]{1,0:T(8,128)} %bitcast.7, f32[512,128]{1,0:T(8,128)} %bitcast.8, bf16[256,256]{1,0:T(8,128)(2,1)} %constant.8.clone.refs_2_, bf16[256,256]{1,0:T(8,128)(2,1)} %constant.9.clone.refs_3_, bf16[128,256]{1,0:T(8,128)(2,1)} %constant.10.clone.refs_4_, ...), custom_call_target="tpu_custom_call" | custom-call | tf_op jit(solution)/shard_map/exchange/pallas_call | solution.py:675
  139.6 0.7 copy.12
  140.3 0.7 copy.13

commit v5 on v4

--- a/solution.py
+++ b/solution.py
@@ -95,7 +95,7 @@
 def kernel(
     nb, nf, n, p_hbm, u_hbm, zf_hbm, zi_hbm, lf_hbm, li_hbm, tab_ref, idx_ref,
     pot_ref, proj_ref,
-    zf_ref, zi_ref, lf_ref, li_ref, pfull, ufull, dbuf, vbuf, d2d, hops, usub, vsub, psub, mine, mrow, mcol, mall,
+    zf_ref, zi_ref, lf_ref, li_ref, p_own, pfull, ufull, dbuf, vbuf, d2d, hops, usub, vsub, psub, mine, mrow, mcol, mall,
     perm_r, loc, agz_r, agx_r, du_r, dv_r, rs_r, many,
 ):
     slab = p_hbm.shape[0]
@@ -166,10 +166,13 @@
             ((zf_hbm, zf_ref), (zi_hbm, zi_ref), (lf_hbm, lf_ref), (li_hbm, li_ref))
         )
     ]
+    p_local = pltpu.make_async_copy(p_hbm, p_own, loc.at[11])
+    p_local.start()
     for table in tables:
         table.start()
     u_local = pltpu.make_async_copy(u_hbm, ufull.at[rows(f * slab, slab)], loc.at[0])
     u_local.start()
+    p_local.wait()
     pl.semaphore_wait(barrier, jnp.where(alone, 5, 7))
 
     def place(at):
@@ -177,14 +180,14 @@
 
     def perm(q):
         return rc(
-            p_hbm.at[rows(q * quarter, quarter)],
+            p_own.at[rows(q * quarter, quarter)],
             pfull.at[rows(to_slot * slab + q * quarter, quarter)],
             perm_s, perm_r.at[q], band=to_band, fft=to_fft,
         )
 
     def perm_here(q):
         return rc(
-            p_hbm.at[rows(q * quarter, quarter)],
+            p_own.at[rows(q * quarter, quarter)],
             pfull.at[rows(place(slot) * slab + q * quarter, quarter)],
             perm_s, perm_r.at[q], band=from_band, fft=from_fft,
         )
@@ -325,19 +328,22 @@
     last = nb // 2
 
     per_slab = planes // batch
+    assert per_slab == 2 and quarters == 4
 
     def items_ready(t):
-        ready = per_slab * (2 * (t // quarters + first - 2) + 1)
-        return jnp.minimum(jnp.minimum(2 * (t + 1), ready), nb * per_slab)
+        q = t % quarters
+        ready = 2 * (2 * (t // quarters + first - 2) + 1) + 2 * ((q + 1) // 2)
+        return jnp.minimum(2 * (t + 1), ready)
 
     first = 5
 
     def items(start, stop):
         @pl.loop(start, stop)
         def _(w):
-            order, k = w // per_slab, w % per_slab
-            far = (order + 1) // 2
-            owner = jnp.where(order % 2 == 1, slot + far, slot - far + nb) % nb
+            far = (w + 2) // 4
+            ends = jnp.logical_or(w < 2, w >= nb * per_slab - 2)
+            k = jnp.where(ends, w % 2, (w - 2) // 2 % 2)
+            owner = jnp.where(ends | (w % 2 == 0), slot + far, slot - far + nb) % nb
             forward_planes(place(owner), k)
 
     @pl.loop(0, quarters * (last + 1 - first))
@@ -392,20 +398,19 @@
     done = items_ready(quarters * (last + 1 - first) - 1)
     before = (nb - 1) * per_slab
 
+    def orbital_parts(start, stop):
+        @pl.loop(start, stop)
+        def _(i):
+            for h in (0, 1):
+                spread(*au, h, farthest_first(i, nb)).start()
+
     @pl.loop(0, 2)
     def _(m):
         @pl.when(m == 1)
         def _():
             for q in range(quarters):
                 agz_here(last, q, 2 * q // quarters).wait_recv()
-
-            @pl.loop(1, nb)
-            def _(i):
-                for h in (0, 1):
-                    spread(*au, h, farthest_first(i, nb)).start()
-
-            for h in (0, 1):
-                u_mine(h).start()
+            orbital_parts(last, nb)
 
         items(jnp.where(m == 0, done, before), jnp.where(m == 0, before, nb * per_slab))
         a = (slot // nf + m) % 2
@@ -435,6 +440,10 @@
                     dbuf[t, :] = field
 
     order = (2, 1, nx - 1, 0)
+
+    orbital_parts(1, last)
+    for h in (0, 1):
+        u_mine(h).start()
 
     def dv(h, k):
         src = vbuf.at[rows(slab_of(order[k], 1 - c) * slab + h * half, half)]
@@ -678,6 +687,7 @@
             in_specs=[any_spec] * 6 + [smem, smem],
             out_specs=(vmem, vmem),
             scratch_shapes=[pltpu.VMEM(t.shape, BF) for t in rest[:4]] + [
+                pltpu.VMEM((slab, width), F32),
                 pltpu.VMEM((nb * slab, width), F32),
                 pltpu.VMEM((nf * slab, width), F32),
                 pltpu.VMEM((2 * n * (n + PAD), width), F32),
@@ -691,7 +701,7 @@
                 pltpu.VMEM((nf, tall, width), F32),
                 pltpu.VMEM((tall, width), F32),
                 pltpu.VMEM((nb, tall, width), F32),
-                dma((4,)), dma((11,)), dma((nb // 2 + 1, 4, 2)), dma((2, 2, 2)), dma((4,)),
+                dma((4,)), dma((12,)), dma((nb // 2 + 1, 4, 2)), dma((2, 2, 2)), dma((4,)),
                 dma((2, 4)), dma((2, 6)), dma((16,)),
             ],
             compiler_params=pltpu.CompilerParams(collective_id=0, has_side_effects=True),

time: 141 us -> 140 us (level)
  no operation moved by 1% of the time
where the time goes in v5:
time: 140 us
  Pallas kernels  138 us (99%)
  local copies, waits for them, and re-layouts  1.41 us (1%)
    pallas_call x1, Pallas kernels, call(): pl.pallas_call(lambda *refs: kernel(nb, nf, n, *refs), out_shape=(out, ou...  138 us

profile of v5, /device:TPU:33, one launch (start us, length us, event | category | flops | bytes accessed | tf_op | source)
XLA Modules:
  0.0 139.8 jit_solution(4979309711817598447)
XLA Ops:
  0.6 137.8 %exchange.1 = (f32[512,128]{1,0:T(8,128)S(1)}, f32[512,128]{1,0:T(8,128)S(1)}) custom-call(f32[512,128]{1,0:T(8,128)} %bitcast.7, f32[512,128]{1,0:T(8,128)} %bitcast.8, bf16[256,256]{1,0:T(8,128)(2,1)} %constant.8.clone.refs_2_, bf16[256,256]{1,0:T(8,128)(2,1)} %constant.9.clone.refs_3_, bf16[128,256]{1,0:T(8,128)(2,1)} %constant.10.clone.refs_4_, ...), custom_call_target="tpu_custom_call" | custom-call | tf_op jit(solution)/shard_map/exchange/pallas_call | solution.py:684
  138.4 0.7 copy.12
  139.1 0.7 copy.13

commit v6 on v5

--- a/solution.py
+++ b/solution.py
@@ -399,7 +399,7 @@
     before = (nb - 1) * per_slab
 
     def orbital_parts(start, stop):
-        @pl.loop(start, stop)
+        @pl.loop(start, stop, unroll=True)
         def _(i):
             for h in (0, 1):
                 spread(*au, h, farthest_first(i, nb)).start()
@@ -537,7 +537,7 @@
             vbuf[own_rows(0, h, 1), :] + hops[landing(h, 2), :] + hops[landing(h, 5), :]
         )
 
-        @pl.loop(1, nb)
+        @pl.loop(1, nb, unroll=True)
         def _(m):
             spread(*av, h, farthest_first(m, nb)).start()
 

time: 140 us -> 140 us (level); the launches traced: 140 us -> 138 us
  Pallas kernels: 138 us -> 136 us
    pallas_call x1, Pallas kernels: 138 us -> 136 us  [call(): pl.pallas_call(lambda *refs: kernel(nb, nf, n, *refs), out_shape=(out, ou...]
where the time goes in v6:
time: 140 us; the launch traced here: 138 us
  Pallas kernels  136 us (97%)
  local copies, waits for them, and re-layouts  1.41 us (1%)
    pallas_call x1, Pallas kernels, call(): pl.pallas_call(lambda *refs: kernel(nb, nf, n, *refs), out_shape=(out, ou...  136 us

profile of v6, /device:TPU:33, one launch (start us, length us, event | category | flops | bytes accessed | tf_op | source)
XLA Modules:
  0.0 138.4 jit_solution(7600122228131742165)
XLA Ops:
  0.6 136.3 %exchange.1 = (f32[512,128]{1,0:T(8,128)S(1)}, f32[512,128]{1,0:T(8,128)S(1)}) custom-call(f32[512,128]{1,0:T(8,128)} %bitcast.7, f32[512,128]{1,0:T(8,128)} %bitcast.8, bf16[256,256]{1,0:T(8,128)(2,1)} %constant.8.clone.refs_2_, bf16[256,256]{1,0:T(8,128)(2,1)} %constant.9.clone.refs_3_, bf16[128,256]{1,0:T(8,128)(2,1)} %constant.10.clone.refs_4_, ...), custom_call_target="tpu_custom_call" | custom-call | tf_op jit(solution)/shard_map/exchange/pallas_call | solution.py:684
  137.0 0.7 copy.12
  137.7 0.7 copy.13
